TPU v7x, 32 devices: a 4x4x1 block of a 4x4x8 slice. The times are simulated.
32 devices in a mesh: dp: 1 (over z), ep: 4 (over y), tp: 8 (over x, core).
Axes of the slice: x: 4, y: 4, z: 1, core: 2. Of those that a mesh axis runs over, the one named last changes fastest.
The devices are a block of a 4x4x8 slice.
Arguments:
- tokens: bfloat16 [32768, 768], P(('dp', 'ep', 'tp'))
- expert_ids: int32 [32768, 1], P(('dp', 'ep', 'tp'))
- gate_vals: float32 [32768, 1], P(('dp', 'ep', 'tp'))
- w_gate: bfloat16 [64, 768, 3072], P('ep', None, 'tp')
- w_up: bfloat16 [64, 768, 3072], P('ep', None, 'tp')
- w_down: bfloat16 [64, 3072, 768], P('ep', 'tp')
Outputs:
- output: bfloat16 [32768, 768], P(('dp', 'ep', 'tp'))
All inputs are finite; a program needn't handle non-finite values.
Results may differ from a plain program's by a relative error of at most 0.00844203.
Values are sent between devices in bfloat16 or wider.
A program may use at most 768 MiB of HBM per device.

v0:
```python
import jax
import jax.numpy as jnp
from jax import lax
from jax.sharding import PartitionSpec as P

CAP_FACTOR = 2


def slot_table(ids_loc, n_exp):
    tok_loc, n_top = ids_loc.shape
    flat_ids = ids_loc.reshape(tok_loc * n_top)
    one_hot = (flat_ids[:, None] == jnp.arange(n_exp, dtype=jnp.int32)[None, :]).astype(jnp.int32)
    preceding = jnp.cumsum(one_hot, axis=0) - one_hot
    return jnp.sum(preceding * one_hot, axis=1).reshape(tok_loc, n_top)


def dispatch_plan(ids_loc, n_exp, capacity):
    tok_loc, n_top = ids_loc.shape
    slot_ids = slot_table(ids_loc, n_exp)
    kept_mask = slot_ids < capacity
    flat_pos = jnp.where(kept_mask, ids_loc * capacity + slot_ids, n_exp * capacity)
    tok_index = jnp.broadcast_to(jnp.arange(tok_loc, dtype=jnp.int32)[:, None], (tok_loc, n_top))
    src_rows = jnp.zeros((n_exp * capacity,), jnp.int32).at[flat_pos.reshape(-1)].set(tok_index.reshape(-1), mode="drop")
    return src_rows, flat_pos, kept_mask


def combine_rows(y_slots, flat_pos, kept_mask, gate_loc):
    picked = jnp.take(y_slots, jnp.where(kept_mask, flat_pos, 0), axis=0)
    weights = jnp.where(kept_mask, gate_loc, 0.0)
    return jnp.sum(picked.astype(jnp.float32) * weights[:, :, None], axis=1)


def solution(mesh):
    expert_ranks = mesh.shape["ep"]
    row_spec = P(("dp", "ep", "tp"), None)

    def local_layer(x_loc, ids_loc, gate_loc, wg_loc, wu_loc, wd_loc):
        tok_loc, d_model = x_loc.shape
        n_top = ids_loc.shape[1]
        local_exp = wg_loc.shape[0]
        n_exp = local_exp * expert_ranks
        capacity = CAP_FACTOR * n_top * tok_loc // n_exp
        src_rows, flat_pos, kept_mask = dispatch_plan(ids_loc, n_exp, capacity)
        send_rows = jnp.take(x_loc, src_rows, axis=0).reshape(expert_ranks, local_exp, capacity, d_model)
        recv_rows = lax.all_to_all(send_rows, "ep", 0, 2, tiled=True)[0]
        group_rows = lax.all_gather(recv_rows, "tp", axis=1, tiled=True)
        gate_pre = jnp.einsum("erd,edf->erf", group_rows, wg_loc, preferred_element_type=jnp.float32)
        up_pre = jnp.einsum("erd,edf->erf", group_rows, wu_loc, preferred_element_type=jnp.float32)
        hidden = (jax.nn.silu(gate_pre) * up_pre).astype(jnp.bfloat16)
        part_sums = jnp.einsum("erf,efd->erd", hidden, wd_loc, preferred_element_type=jnp.float32).astype(jnp.bfloat16)
        pieces = lax.all_to_all(part_sums[None], "tp", 2, 0, tiled=True)
        y_rows = jnp.sum(pieces.astype(jnp.float32), axis=0).astype(jnp.bfloat16)
        returned = lax.all_to_all(y_rows[None], "ep", 2, 0, tiled=True)
        y_slots = returned.reshape(n_exp * capacity, d_model)
        return combine_rows(y_slots, flat_pos, kept_mask, gate_loc).astype(jnp.bfloat16)

    return jax.shard_map(local_layer, mesh=mesh, in_specs=(row_spec, row_spec, row_spec, P("ep", None, "tp"), P("ep", None, "tp"), P("ep", "tp", None)), out_specs=row_spec, check_vma=False)
```

profile of v0, /device:TPU:97, one launch (start us, length us, event | category | flops | bytes accessed | tf_op | source)
XLA Modules:
  0.0 653.7 jit_solution(9568028532847903110)
XLA Ops:
  6.5 0.0 copy-start
  6.6 0.0 all-gather.2.cloned.1.call-start
  6.6 0.8 fusion.6
  7.4 18.0 %reduce-window.6 = s32[64,8,128]{2,1,0:T(8,128)S(1)} reduce-window(s32[64,8,128]{2,1,0:T(8,128)S(1)} %fusion.6, s32[]{:T(128)} %constant.25.clone.1), window={size=1x1x128 pad=0_0x0_0x127_0}, to_apply=%region_0.0 | reduce-window | flops 8323072 | bytes 524292 | tf_op jit(solution)/shard_map/reduce-window
  25.4 0.1 slice.12
  25.5 0.1 copy.13
  25.7 0.1 copy.14
  25.8 0.1 broadcast_add_fusion
  25.9 0.8 fusion.5
  26.7 0.7 compare_select_fusion
  27.4 4.3 scatter_custom_fusion
  31.8 0.1 broadcast_in_dim.56
  31.9 0.0 copy-done
  31.9 9.4 %gather_fusion = bf16[2048,768]{1,0:T(8,128)(2,1)} fusion(bf16[1024,768]{1,0:T(8,128)(2,1)S(1)} %copy-done, s32[2048]{0:T(1024)S(1)} %fusion.7), kind=kCustom, calls=%fused_computation | custom fusion | bytes 6299648 | tf_op jit(solution)/shard_map/jit(_take)/gather | solution.py:44
  41.2 2.1 broadcast_select_fusion
  43.4 42.9 %all_to_all.42 = bf16[4,16,32,768]{3,2,1,0:T(8,128)(2,1)S(1)} all-to-all(bf16[4,16,32,768]{3,2,1,0:T(8,128)(2,1)S(1)} %broadcast_select_fusion), channel_id=1, replica_groups=mesh['dp'=1,'ep'=4,'tp'=8] {'ep'}, dimensions={0} | all-to-all | bytes 6291456 | tf_op jit(solution)/shard_map/all_to_all | solution.py:45
  86.3 2.0 copy.15
  88.3 0.1 all-gather.2.cloned.1.call-update
  88.4 119.7 %all-gather.2.cloned.1.call-done = bf16[16,1024,768]{2,1,0:T(8,128)(2,1)} async-done(((bf16[16,128,768]{2,1,0:T(8,128)(2,1)}), bf16[16,1024,768]{2,1,0:T(8,128)(2,1)}) %all-gather.2.cloned.1.call-update) | async-done | bytes 25165840 | tf_op jit(solution)/shard_map/all_gather | solution.py:46
  208.1 26.9 %fusion.11 = f32[16,1024,384]{2,1,0:T(8,128)} fusion(bf16[16,1024,768]{2,1,0:T(8,128)(2,1)} %all-gather.2.cloned.1.call-done, bf16[16,768,384]{2,1,0:T(8,128)(2,1)} %param.9), kind=kOutput, calls=%fused_computation.30 | convolution fusion | flops 9663676416 | bytes 59768832 | tf_op jit(solution)/shard_map/erd,edf->erf/dot_general | solution.py:47
  235.0 40.7 %convert_bitcast_fusion = bf16[1,16,1024,768]{3,2,1,0:T(8,128)(2,1)} fusion(bf16[16,384,768]{2,1,0:T(8,128)(2,1)} %param.11, f32[16,1024,384]{2,1,0:T(8,128)} %fusion.11, bf16[16,1024,768]{2,1,0:T(8,128)(2,1)} %all-gather.2.cloned.1.call-done, bf16[16,768,384]{2,1,0:T(8,128)(2,1)} %param.10), kind=kOutput, calls=%fused_computation.3 | convolution fusion | flops 19377684480 | bytes 94371840 | tf_op jit(solution)/shard_map/erf,efd->erd/dot_general | solution.py:50
  275.7 23.2 %copy.16 = bf16[1,16,1024,768]{3,1,0,2:T(8,128)(2,1)S(1)} copy(bf16[1,16,1024,768]{3,2,1,0:T(8,128)(2,1)} %convert_bitcast_fusion) | data formatting | bytes 50331648 | tf_op jit(solution)/shard_map/broadcast_in_dim | solution.py:51
  299.0 277.8 %all_to_all.43 = bf16[1,16,1024,768]{3,1,0,2:T(8,128)(2,1)} all-to-all(bf16[1,16,1024,768]{3,1,0,2:T(8,128)(2,1)S(1)} %copy.16), channel_id=1, replica_groups=mesh['dp'=1,'ep'=4,'tp'=8] {'tp'}, dimensions={2} | all-to-all | bytes 50331648 | tf_op jit(solution)/shard_map/all_to_all | solution.py:51
  576.8 0.0 copy-start.2
  576.8 0.0 copy-start.3
  576.8 15.6 %reduce_sum.29 = bf16[16,128,768]{2,0,1:T(8,128)(2,1)} reduce(bf16[16,8,128,768]{3,0,2,1:T(8,128)(2,1)} %bitcast.48, bf16[]{:T(256)} %constant.46.clone.1), dimensions={1}, to_apply=%region_4.5 | reduce | flops 11010048 | bytes 28311554 | tf_op jit(solution)/shard_map/reduce_sum | solution.py:52
  592.5 4.7 all-to-all-start.2
  597.2 0.0 copy-done.2
  597.2 0.0 copy-done.3
  597.3 36.3 %all-to-all-done.2 = bf16[1,16,128,768]{3,1,0,2:T(8,128)(2,1)} async-done(((bf16[1,16,128,768]{3,1,0,2:T(8,128)(2,1)}), bf16[1,16,128,768]{3,1,0,2:T(8,128)(2,1)}, u32[]{:S(2)}, u32[]{:S(2)}) %all-to-all-start.2) | async-done | bytes 3145760 | tf_op jit(solution)/shard_map/all_to_all | solution.py:53
  633.6 2.9 copy.17
  636.5 0.0 copy-start.1
  636.5 1.9 copy.18
  638.4 6.8 %gather_fusion.1 = bf16[1024,768]{1,0:T(8,128)(2,1)S(1)} fusion(bf16[2048,768]{1,0:T(8,128)(2,1)} %bitcast.49, s32[1024]{0:T(1024)S(1)} %broadcast_clamp_fusion), kind=kCustom, calls=%fused_computation.1 | custom fusion | bytes 3149824 | tf_op jit(solution)/shard_map/jit(_take)/gather | solution.py:28
  645.2 1.6 multiply_convert_fusion.2
  646.8 0.0 copy-done.1
  (8 shorter events, 0.1 us)
Async XLA Ops:
  6.5 25.3 %copy-start = (bf16[1024,768]{1,0:T(8,128)(2,1)S(1)}, bf16[1024,768]{1,0:T(8,128)(2,1)}, u32[]{:S(2)}) copy-start(bf16[1024,768]{1,0:T(8,128)(2,1)} %param.6) | copy-start | bytes 4718596
  6.6 201.5 %all-gather.2.cloned.1.call-start = ((), (), s32[]{:S(2)}) async-start(), calls=%async_computation.3 | async-start | bytes 28311552 | tf_op jit(solution)/shard_map/all_gather | solution.py:46
  576.8 20.3 %copy-start.2 = (s32[1024,1]{0,1:T(1,128)S(1)}, s32[1024,1]{0,1:T(1,128)}, u32[]{:S(2)}) copy-start(s32[1024,1]{0,1:T(1,128)} %param.7) | copy-start | bytes 12292
  576.8 20.4 %copy-start.3 = (f32[1024,1]{0,1:T(1,128)S(1)}, f32[1024,1]{0,1:T(1,128)}, u32[]{:S(2)}) copy-start(f32[1024,1]{0,1:T(1,128)} %param.8) | copy-start | bytes 12292
  592.5 41.1 %all-to-all-start.2 = ((bf16[1,16,128,768]{3,1,0,2:T(8,128)(2,1)}), bf16[1,16,128,768]{3,1,0,2:T(8,128)(2,1)}, u32[]{:S(2)}, u32[]{:S(2)}) async-start(bf16[1,16,128,768]{3,1,0,2:T(8,128)(2,1)} %bitcast.53), calls=%async_computation.2 | async-start | bytes 6291456 | tf_op jit(solution)/shard_map/all_to_all | solution.py:53
  636.5 10.3 %copy-start.1 = (bf16[1024,768]{1,0:T(8,128)(2,1)S(1)}, bf16[1024,768]{1,0:T(8,128)(2,1)}, u32[]{:S(2)}) copy-start(bf16[1024,768]{1,0:T(8,128)(2,1)} %param.6) | copy-start | bytes 4718596
Sparse Core Ops, SparseCore 0:
  88.5 119.5 all-gather.1
where the time goes:
time: 654 us
  blocking collectives  321 us (49%)
  waiting for transfers between devices  156 us (24%)
  matrix products  67.6 us (10%)
  local copies, waits for them, and re-layouts  51 us (8%)
  other arithmetic  39.8 us (6%)
  between operations  13.6 us (2%)
    all_to_all x1, blocking collectives, local_layer(): pieces = lax.all_to_all(part_sums[None], 'tp', 2, 0, tiled=True)  278 us
    all_gather x1, waiting for transfers between devices, local_layer(): group_rows = lax.all_gather(recv_rows, 'tp', axis=1, tiled=True)  120 us
    all_to_all x1, blocking collectives, local_layer(): recv_rows = lax.all_to_all(send_rows, 'ep', 0, 2, tiled=True)[0]  42.9 us
    dot_general x1, matrix products, local_layer(): jnp.einsum('erf,efd->erd', hidden, wd_loc, preferred_element_type=jnp.flo...  40.7 us
    all_to_all x1, waiting for transfers between devices, local_layer(): returned = lax.all_to_all(y_rows[None], 'ep', 2, 0, tiled=True)  36.3 us
    dot_general x1, matrix products, local_layer(): jnp.einsum('erd,edf->erf', group_rows, wg_loc, preferred_element_type=jnp...  26.9 us
    broadcast_in_dim x1, local copies, waits for them, and re-layouts, local_layer(): pieces = lax.all_to_all(part_sums[None], 'tp', 2, 0, tiled=True)  23.2 us
    another operation x3, other arithmetic  18.2 us
  transfers between devices with their start and end apart: 2, of which 2 were waited for; matrix products, arithmetic and copies ran while one was open for 0% of the time, Pallas kernels for 0%

commit v1 on v0

v1 whole, which is shorter than its diff:
```python
import functools

import jax
import jax.numpy as jnp
from jax import lax
from jax.experimental import pallas as pl
from jax.experimental.pallas import tpu as pltpu
from jax.sharding import PartitionSpec as P

CAP_FACTOR = 2
GROUP = 2
MESH = pl.DeviceIdType.MESH
BF16 = jnp.bfloat16
F32 = jnp.float32


def dispatch_kernel(capacity, n_exp, ids_ref, x_ref, rows_ref, pos_ref):
    tok = ids_ref.shape[1]
    n_slots = rows_ref.shape[0]
    ids = ids_ref[...]
    one_hot = lax.broadcasted_iota(jnp.int32, (n_exp, tok), 0) == ids
    before = lax.broadcasted_iota(jnp.int32, (tok, tok), 0) < lax.broadcasted_iota(jnp.int32, (tok, tok), 1)
    preceding = jnp.dot(one_hot.astype(F32).astype(BF16), before.astype(F32).astype(BF16), preferred_element_type=F32)
    slot = jnp.sum(jnp.where(one_hot, preceding, 0.0), axis=0, keepdims=True).astype(jnp.int32)
    pos = jnp.where(slot < capacity, ids * capacity + slot, -1)
    pos_ref[...] = pos
    tile = 256

    @pl.loop(0, n_slots // tile)
    def _(i):
        want = lax.broadcasted_iota(jnp.int32, (tile, tok), 0) + i * tile
        pick = (want == pos).astype(F32).astype(BF16)
        start = pl.multiple_of(i * tile, tile)
        rows_ref[pl.ds(start, tile), :] = jnp.dot(pick, x_ref[...], preferred_element_type=F32).astype(BF16)


def dispatch(x_loc, ids_loc, n_exp, capacity):
    tok, d_model = x_loc.shape
    return pl.pallas_call(
        functools.partial(dispatch_kernel, capacity, n_exp),
        out_shape=(
            jax.ShapeDtypeStruct((n_exp * capacity, d_model), BF16),
            jax.ShapeDtypeStruct((1, tok), jnp.int32),
        ),
        name="dispatch",
    )(ids_loc.reshape(1, tok), x_loc)


def combine_kernel(pos_ref, gate_ref, y_ref, out_ref):
    n_slots = y_ref.shape[0]
    tok = out_ref.shape[0]
    tile = 256

    @pl.loop(0, tok // tile)
    def _(i):
        rows = pl.ds(pl.multiple_of(i * tile, tile), tile)
        pos = pos_ref[rows, :]
        pick = (lax.broadcasted_iota(jnp.int32, (tile, n_slots), 1) == pos).astype(F32).astype(BF16)
        y = jnp.dot(pick, y_ref[...], preferred_element_type=F32)
        weight = jnp.where(pos >= 0, gate_ref[rows, :], 0.0)
        out_ref[rows, :] = (y * weight).astype(BF16)


def combine(pos, gate_loc, y_slots):
    tok = gate_loc.shape[0]
    return pl.pallas_call(
        combine_kernel,
        out_shape=jax.ShapeDtypeStruct((tok, y_slots.shape[1]), BF16),
        name="combine",
    )(pos.reshape(tok, 1), gate_loc, y_slots)


def expert_kernel(
    n_y, n_x, rows_hbm, wg_hbm, wu_hbm, wd_hbm, out_hbm,
    x_buf, pair_buf, opp_buf, nbr_buf, w_in, w_out,
    ys_send, ys_recv, ys_loc, a_send, a_recv, b_send, b_recv, d_send, d_recv,
    p_send, p_recv, e_send, e_recv, f_send, f_recv, h_send, h_recv, h_loc, w_sem,
):
    n_loc, _, _, cap, d_model = x_buf.shape
    hidden = w_out.shape[2]
    n_grp = n_loc // GROUP
    half = n_y // 2
    yy = lax.axis_index("ep")
    tt = lax.axis_index("tp")
    xx, cc = tt // 2, tt % 2
    xr, xl, xo = (xx + 1) % n_x, (xx + n_x - 1) % n_x, (xx + 2) % n_x
    right, left, mate = {"tp": xr * 2 + cc}, {"tp": xl * 2 + cc}, {"tp": xx * 2 + 1 - cc}
    peers = [(yy + d) % n_y for d in range(1, n_y)]
    mine = cc * n_x

    def remote(src, dst, send, recv, device):
        return pltpu.make_async_remote_copy(
            src_ref=src, dst_ref=dst, send_sem=send, recv_sem=recv, device_id=device, device_id_type=MESH
        )

    def grp(g):
        return pl.ds(g * GROUP, GROUP)

    def y_copy(g, k, peer):
        return remote(
            rows_hbm.at[pl.ds(peer * n_loc + g * GROUP, GROUP)], x_buf.at[grp(g), mine + xx, yy],
            ys_send.at[g, k], ys_recv.at[g, k], {"ep": peer},
        )

    def y_local(g):
        return pltpu.make_async_copy(
            rows_hbm.at[pl.ds(yy * n_loc + g * GROUP, GROUP)], x_buf.at[grp(g), mine + xx, yy], ys_loc.at[g]
        )

    def block_copy(g, blk, send, recv, device):
        view = x_buf.at[grp(g), mine + blk]
        return remote(view, view, send, recv, device)

    def a_copy(g, k):
        return block_copy(g, xx, a_send.at[g, k], a_recv.at[g, k], (right, left)[k])

    def b_copy(g, k):
        view = x_buf.at[grp(g), mine + (xl, xr)[k], pl.ds(k * half, half)]
        return remote(view, view, b_send.at[g, k], b_recv.at[g, k], (right, left)[k])

    def d_copy(g, k):
        return block_copy(g, (xx, xl, xr, xo)[k], d_send.at[g, k], d_recv.at[g, k], mate)

    def p_copy(g):
        other = (1 - cc) * n_x
        return remote(x_buf.at[grp(g), pl.ds(other, n_x)], pair_buf.at[grp(g)], p_send.at[g], p_recv.at[g], mate)

    def e_copy(g, k):
        view = x_buf.at[grp(g), mine + xo, pl.ds(k * half, half)]
        return remote(view, opp_buf.at[k, grp(g)], e_send.at[g, k], e_recv.at[g, k], (right, left)[k])

    def f_copy(g, k):
        view = x_buf.at[grp(g), mine + (xr, xl)[k]]
        return remote(view, nbr_buf.at[k, grp(g)], f_send.at[g, k], f_recv.at[g, k], (right, left)[k])

    def h_copy(g, k, peer):
        return remote(
            x_buf.at[grp(g), mine + xx, peer], out_hbm.at[pl.ds(yy * n_loc + g * GROUP, GROUP)],
            h_send.at[g, k], h_recv.at[g, k], {"ep": peer},
        )

    def h_local(g):
        return pltpu.make_async_copy(
            x_buf.at[grp(g), mine + xx, yy], out_hbm.at[pl.ds(yy * n_loc + g * GROUP, GROUP)], h_loc.at[g]
        )

    def w_copies(g):
        s = g % 2
        return (
            pltpu.make_async_copy(wg_hbm.at[grp(g)], w_in.at[s, :, :, pl.ds(0, hidden)], w_sem.at[s, 0]),
            pltpu.make_async_copy(wu_hbm.at[grp(g)], w_in.at[s, :, :, pl.ds(hidden, hidden)], w_sem.at[s, 1]),
            pltpu.make_async_copy(wd_hbm.at[grp(g)], w_out.at[s], w_sem.at[s, 2]),
        )

    for g in range(2):
        for c in w_copies(g):
            c.start()

    barrier = pltpu.get_barrier_semaphore()
    for device in [right, left, mate] + [{"ep": p} for p in peers]:
        pl.semaphore_signal(barrier, inc=1, device_id=device, device_id_type=MESH)
    pl.semaphore_wait(barrier, 3 + len(peers))

    @pl.loop(0, n_grp)
    def _(g):
        for k, peer in enumerate(peers):
            y_copy(g, k, peer).start()
        y_local(g).start()

    def stage_a(g):
        for k, peer in enumerate(peers):
            y_copy(g, k, peer).wait_recv()
        y_local(g).wait()
        for k in range(2):
            a_copy(g, k).start()
        d_copy(g, 0).start()

    def stage_b(g):
        for k in range(2):
            a_copy(g, k).wait_recv()
            b_copy(g, k).start()
        for k in range(2):
            d_copy(g, 1 + k).start()

    def stage_c(g):
        for k in range(2):
            b_copy(g, k).wait_recv()
        d_copy(g, 3).start()

    def stage_d(g):
        for k in range(4):
            d_copy(g, k).wait()
        for k in range(2):
            a_copy(g, k).wait_send()
            b_copy(g, k).wait_send()
        for c in w_copies(g):
            c.wait()
        s = g % 2
        blocks = 2
        per = 2 * n_x // blocks

        @pl.loop(0, GROUP * per)
        def _(j):
            el = j // per
            at = (g * GROUP + el, pl.ds((j % per) * blocks, blocks))
            tile = x_buf[at].reshape(blocks * n_y * cap, d_model)
            both = jnp.dot(tile, w_in[s, el], preferred_element_type=F32)
            pre = both[:, :hidden]
            act = (jax.nn.silu(pre) * both[:, hidden:]).astype(BF16)
            part = jnp.dot(act, w_out[s, el], preferred_element_type=F32)
            x_buf[at] = part.astype(BF16).reshape(blocks, n_y, cap, d_model)

        p_copy(g).start()

        @pl.when(g + 2 < n_grp)
        def _():
            for c in w_copies(g + 2):
                c.start()

    def stage_e(g):
        p_copy(g).wait_recv()

        @pl.loop(0, GROUP * n_y)
        def _(j):
            e, q = g * GROUP + j // n_y, j % n_y
            total = x_buf[e, mine + xo, q].astype(F32) + pair_buf[e, xo, q].astype(F32)
            x_buf[e, mine + xo, q] = total.astype(BF16)

        for k in range(2):
            e_copy(g, k).start()

    def stage_f(g):
        for k in range(2):
            e_copy(g, k).wait_recv()
            blk = (xr, xl)[k]

            @pl.loop(0, GROUP * half)
            def _(j):
                e, q = g * GROUP + j // half, j % half
                a = q + k * half
                total = x_buf[e, mine + blk, a].astype(F32) + pair_buf[e, blk, a].astype(F32)
                total = total + opp_buf[k, e, q].astype(F32)
                x_buf[e, mine + blk, a] = total.astype(BF16)
                b = q + (1 - k) * half
                rest = x_buf[e, mine + blk, b].astype(F32) + pair_buf[e, blk, b].astype(F32)
                x_buf[e, mine + blk, b] = rest.astype(BF16)

            f_copy(g, k).start()

    def stage_h(g):
        for k in range(2):
            f_copy(g, k).wait_recv()

        @pl.loop(0, GROUP * n_y)
        def _(j):
            e, q = g * GROUP + j // n_y, j % n_y
            total = x_buf[e, mine + xx, q].astype(F32) + pair_buf[e, xx, q].astype(F32)
            total = total + (nbr_buf[0, e, q].astype(F32) + nbr_buf[1, e, q].astype(F32))
            x_buf[e, mine + xx, q] = total.astype(BF16)

        for k, peer in enumerate(peers):
            h_copy(g, k, peer).start()
        h_local(g).start()

    stages = (stage_a, stage_b, stage_c, stage_d, stage_e, stage_f, stage_h)

    @pl.loop(0, n_grp + len(stages) - 1)
    def _(t):
        for lag, stage in enumerate(stages):
            g = t - lag

            @pl.when((g >= 0) & (g < n_grp))
            def _():
                stage(g)

    @pl.loop(0, n_grp)
    def _(g):
        p_copy(g).wait_send()
        for k in range(2):
            e_copy(g, k).wait_send()
            f_copy(g, k).wait_send()
        for k, peer in enumerate(peers):
            y_copy(g, k, peer).wait_send()
            h_copy(g, k, peer).wait()
        h_local(g).wait()


def experts(rows, wg, wu, wd, n_y, n_tp):
    n_exp, cap, d_model = rows.shape
    n_loc, _, hidden = wg.shape
    n_x = n_tp // 2
    half = n_y // 2
    n_grp = n_loc // GROUP
    dma = pltpu.SemaphoreType.DMA
    hbm = pl.BlockSpec(memory_space=pltpu.HBM)
    return pl.pallas_call(
        functools.partial(expert_kernel, n_y, n_x),
        out_shape=jax.ShapeDtypeStruct(rows.shape, BF16),
        in_specs=[hbm] * 4,
        out_specs=hbm,
        scratch_shapes=[
            pltpu.VMEM((n_loc, 2 * n_x, n_y, cap, d_model), BF16),
            pltpu.VMEM((n_loc, n_x, n_y, cap, d_model), BF16),
            pltpu.VMEM((2, n_loc, half, cap, d_model), BF16),
            pltpu.VMEM((2, n_loc, n_y, cap, d_model), BF16),
            pltpu.VMEM((2, GROUP, d_model, 2 * hidden), BF16),
            pltpu.VMEM((2, GROUP, hidden, d_model), BF16),
            dma((n_grp, n_y - 1)), dma((n_grp, n_y - 1)), dma((n_grp,)),
            dma((n_grp, 2)), dma((n_grp, 2)),
            dma((n_grp, 2)), dma((n_grp, 2)),
            dma((n_grp, 4)), dma((n_grp, 4)),
            dma((n_grp,)), dma((n_grp,)),
            dma((n_grp, 2)), dma((n_grp, 2)),
            dma((n_grp, 2)), dma((n_grp, 2)),
            dma((n_grp, n_y - 1)), dma((n_grp, n_y - 1)), dma((n_grp,)),
            dma((2, 3)),
        ],
        compiler_params=pltpu.CompilerParams(
            collective_id=0, has_side_effects=True, vmem_limit_bytes=67043328
        ),
        name="experts",
    )(rows, wg, wu, wd)


def solution(mesh):
    n_y, n_tp = mesh.shape["ep"], mesh.shape["tp"]
    row_spec = P(("dp", "ep", "tp"), None)

    def local_layer(x_loc, ids_loc, gate_loc, wg_loc, wu_loc, wd_loc):
        tok, d_model = x_loc.shape
        n_exp = wg_loc.shape[0] * n_y
        capacity = CAP_FACTOR * tok // n_exp
        rows, pos = dispatch(x_loc, ids_loc, n_exp, capacity)
        y = experts(rows.reshape(n_exp, capacity, d_model), wg_loc, wu_loc, wd_loc, n_y, n_tp)
        return combine(pos, gate_loc, y.reshape(n_exp * capacity, d_model))

    return jax.shard_map(local_layer, mesh=mesh, in_specs=(row_spec, row_spec, row_spec, P("ep", None, "tp"), P("ep", None, "tp"), P("ep", "tp", None)), out_specs=row_spec, check_vma=False)
```

time: 654 us -> 244 us (0.37)
  blocking collectives: 321 us -> 0 us
  Pallas kernels: 0 us -> 239 us
  waiting for transfers between devices: 156 us -> 0 us
  matrix products: 67.6 us -> 0 us
  local copies, waits for them, and re-layouts: 51 us -> 3.43 us
  other arithmetic: 39.8 us -> 0 us
  between operations: 13.6 us -> 0.01 us
    all_to_all x2 -> x0, blocking collectives: 321 us -> none  [the longest x1 278 us: local_layer(): pieces = lax.all_to_all(part_sums[None], 'tp', 2, 0, tiled=True)]
    pallas_call x0 -> x3, Pallas kernels: none -> 239 us  [the longest x1 223 us: experts(): pl.pallas_call(functools.partial(expert_kernel, n_y, n_x), out_shape=jax....]
    all_gather x1 -> x0, waiting for transfers between devices: 120 us -> none  [local_layer(): group_rows = lax.all_gather(recv_rows, 'tp', axis=1, tiled=True)]
    dot_general x2 -> x0, matrix products: 67.6 us -> none  [the longest x1 40.7 us: local_layer(): jnp.einsum('erf,efd->erd', hidden, wd_loc, preferred_element_type=jnp.flo...]
    all_to_all x1 -> x0, waiting for transfers between devices: 36.3 us -> none  [local_layer(): returned = lax.all_to_all(y_rows[None], 'ep', 2, 0, tiled=True)]
    broadcast_in_dim x2 -> x0, local copies, waits for them, and re-layouts: 23.3 us -> none  [the longest x1 23.2 us: local_layer(): pieces = lax.all_to_all(part_sums[None], 'tp', 2, 0, tiled=True)]
    another operation x3 -> x0, other arithmetic: 18.2 us -> none
    reduce_sum x2 -> x0, other arithmetic: 16.4 us -> none  [the longest x1 15.6 us: local_layer(): y_rows = jnp.sum(pieces.astype(jnp.float32), axis=0).astype(jnp.bfloat16)]
  transfers between devices with their start and end apart: 2 -> 0, of which waited for: 2 -> 0; matrix products, arithmetic and copies ran while one was open for 0% -> 0% of each run, Pallas kernels for 0% -> 0%
where the time goes in v1:
time: 244 us; the launch traced here: 242 us
  Pallas kernels  239 us (98%)
  local copies, waits for them, and re-layouts  3.43 us (1%)
    pallas_call x1, Pallas kernels, experts(): pl.pallas_call(functools.partial(expert_kernel, n_y, n_x), out_shape=jax....  223 us
    pallas_call x1, Pallas kernels, dispatch(): pl.pallas_call(functools.partial(dispatch_kernel, capacity, n_exp), out_s...  8.13 us
    pallas_call x1, Pallas kernels, combine(): pl.pallas_call(combine_kernel, out_shape=jax.ShapeDtypeStruct((tok, y_slo...  7.48 us

profile of v1, /device:TPU:97, one launch (start us, length us, event | category | flops | bytes accessed | tf_op | source)
XLA Modules:
  0.0 242.4 jit_solution(9342415117894670479)
XLA Ops:
  0.0 8.1 %dispatch.1 = (bf16[2048,768]{1,0:T(8,128)(2,1)}, s32[1,1024]{1,0:T(1,128)}) custom-call(s32[1,1024]{1,0:T(1,128)} %bitcast.6, bf16[1024,768]{1,0:T(8,128)(2,1)} %x_ref.1), custom_call_target="tpu_custom_call" | custom-call | tf_op jit(solution)/shard_map/dispatch/pallas_call | solution.py:39
  8.1 223.4 %experts.1 = bf16[64,32,768]{2,1,0:T(8,128)(2,1)} custom-call(bf16[64,32,768]{2,1,0:T(8,128)(2,1)} %bitcast.5, bf16[16,768,384]{2,1,0:T(8,128)(2,1)} %wg_hbm.1, bf16[16,768,384]{2,1,0:T(8,128)(2,1)} %wu_hbm.1, bf16[16,384,768]{2,1,0:T(8,128)(2,1)} %wd_hbm.1), custom_call_target="tpu_custom_call" | custom-call | tf_op jit(solution)/shard_map/experts/pallas_call | solution.py:296
  231.5 1.7 copy.8.pos_ref
  233.2 1.7 copy.9.gate_ref
  234.9 7.5 %combine.1 = bf16[1024,768]{1,0:T(8,128)(2,1)} custom-call(s32[1024,1]{1,0:T(8,128)} %copy.8.pos_ref, f32[1024,1]{1,0:T(8,128)} %copy.9.gate_ref, bf16[2048,768]{1,0:T(8,128)(2,1)} %bitcast.4), custom_call_target="tpu_custom_call" | custom-call | tf_op jit(solution)/shard_map/combine/pallas_call | solution.py:66

commit v2 on v1

--- a/solution.py
+++ b/solution.py
@@ -9,6 +9,7 @@
 
 CAP_FACTOR = 2
 GROUP = 2
+W_SLOTS = 4
 MESH = pl.DeviceIdType.MESH
 BF16 = jnp.bfloat16
 F32 = jnp.float32
@@ -322,16 +323,476 @@
     )(rows, wg, wu, wd)
 
 
+def route_kernel(
+    n_y, n_tp, n_exp, capacity, ids_ref, x_ref, rows_ref, pos_ref, table_ref, most_ref,
+    meta, col_send, col_recv, row_send, row_recv,
+):
+    tok = ids_ref.shape[1]
+    packed = rows_ref.shape[1]
+    width = table_ref.shape[2]
+    n_loc = n_exp // n_y
+    yy = lax.axis_index("ep")
+    tt = lax.axis_index("tp")
+    y_peers = [(yy + d) % n_y for d in range(1, n_y)]
+    t_peers = [(tt + d) % n_tp for d in range(1, n_tp)]
+
+    barrier = pltpu.get_barrier_semaphore()
+    for device in [{"ep": p} for p in y_peers] + [{"tp": p} for p in t_peers]:
+        pl.semaphore_signal(barrier, inc=1, device_id=device, device_id_type=MESH)
+
+    ids = ids_ref[...]
+    one_hot = lax.broadcasted_iota(jnp.int32, (n_exp, tok), 0) == ids
+    before = lax.broadcasted_iota(jnp.int32, (tok, tok), 0) < lax.broadcasted_iota(jnp.int32, (tok, tok), 1)
+    before = before.astype(F32).astype(BF16)
+    preceding = jnp.dot(one_hot.astype(F32).astype(BF16), before, preferred_element_type=F32)
+    slot = jnp.sum(jnp.where(one_hot, preceding, 0.0), axis=0, keepdims=True)
+    kept = slot < capacity
+    rank = ids // n_loc
+    pad = 8
+    to_rank = (lax.broadcasted_iota(jnp.int32, (pad, tok), 0) == rank) & kept
+    ahead = jnp.dot(to_rank.astype(F32).astype(BF16), before, preferred_element_type=F32)
+    place = jnp.sum(jnp.where(to_rank, ahead, 0.0), axis=0, keepdims=True).astype(jnp.int32)
+    counts = jnp.sum(to_rank.astype(F32), axis=1, keepdims=True)
+    most = jnp.max(counts, axis=0, keepdims=True).astype(jnp.int32)
+    fits = kept & (place < packed)
+    pos_ref[...] = jnp.where(fits, rank * packed + place, -1)
+    key = jnp.where(fits, rank * tok + place, -1)
+    row_id = lax.broadcasted_iota(jnp.int32, (pad, tok), 0)
+    parts = jnp.where(row_id == 0, (ids % n_loc).astype(F32), jnp.where(row_id == 1, slot, 1.0))
+    parts = jnp.where(kept, parts, 0.0).astype(BF16)
+
+    def pick(r):
+        return ((lax.broadcasted_iota(jnp.int32, (packed, tok), 0) + r * tok) == key).astype(F32).astype(BF16)
+
+    @pl.loop(0, n_y)
+    def _(r):
+        got = lax.dot_general(parts, pick(r), (((1,), (1,)), ((), ())), preferred_element_type=F32)
+        where = jnp.where(got[2:3] > 0.5, got[0:1] * capacity + got[1:2], -1.0)
+        meta[r, :, 0:packed] = where.astype(jnp.int32)
+        meta[r, :, packed:width] = jnp.broadcast_to(most, (1, width - packed))
+
+    pl.semaphore_wait(barrier, len(y_peers) + len(t_peers))
+    table_ref[pl.ds(tt * n_y + yy, 1)] = meta[pl.ds(yy, 1)]
+
+    def col_copy(k):
+        return pltpu.make_async_remote_copy(
+            src_ref=meta.at[y_peers[k]], dst_ref=table_ref.at[tt * n_y + yy],
+            send_sem=col_send.at[k], recv_sem=col_recv.at[k], device_id={"ep": y_peers[k]}, device_id_type=MESH,
+        )
+
+    def col_arrival(k):
+        src = (yy + n_y - 1 - k) % n_y
+        return pltpu.make_async_remote_copy(
+            src_ref=meta.at[src], dst_ref=table_ref.at[tt * n_y + src],
+            send_sem=col_send.at[k], recv_sem=col_recv.at[k], device_id={"ep": src}, device_id_type=MESH,
+        )
+
+    def row_copy(k):
+        view = table_ref.at[pl.ds(tt * n_y, n_y)]
+        return pltpu.make_async_remote_copy(
+            src_ref=view, dst_ref=view,
+            send_sem=row_send.at[k], recv_sem=row_recv.at[k], device_id={"tp": t_peers[k]}, device_id_type=MESH,
+        )
+
+    def row_arrival(k):
+        src = (tt + n_tp - 1 - k) % n_tp
+        view = table_ref.at[pl.ds(src * n_y, n_y)]
+        return pltpu.make_async_remote_copy(
+            src_ref=view, dst_ref=view,
+            send_sem=row_send.at[k], recv_sem=row_recv.at[k], device_id={"tp": src}, device_id_type=MESH,
+        )
+
+    for k in range(len(y_peers)):
+        col_copy(k).start()
+
+    @pl.loop(0, n_y)
+    def _(r):
+        rows_ref[r] = jnp.dot(pick(r), x_ref[...], preferred_element_type=F32).astype(BF16)
+
+    for k in range(len(y_peers)):
+        col_arrival(k).wait_recv()
+    for k in range(len(t_peers)):
+        row_copy(k).start()
+    for k in range(len(t_peers)):
+        row_arrival(k).wait_recv()
+    most_ref[...] = jnp.max(table_ref[:, :, packed:width], axis=0)
+    for k in range(len(y_peers)):
+        col_copy(k).wait_send()
+    for k in range(len(t_peers)):
+        row_copy(k).wait_send()
+
+
+def route(x_loc, ids_loc, n_exp, capacity, packed, n_y, n_tp):
+    tok, d_model = x_loc.shape
+    width = -(-(packed + 1) // 128) * 128
+    dma = pltpu.SemaphoreType.DMA
+    return pl.pallas_call(
+        functools.partial(route_kernel, n_y, n_tp, n_exp, capacity),
+        out_shape=(
+            jax.ShapeDtypeStruct((n_y, packed, d_model), BF16),
+            jax.ShapeDtypeStruct((1, tok), jnp.int32),
+            jax.ShapeDtypeStruct((n_y * n_tp, 1, width), jnp.int32),
+            jax.ShapeDtypeStruct((1, width - packed), jnp.int32),
+        ),
+        scratch_shapes=[
+            pltpu.VMEM((n_y, 1, width), jnp.int32),
+            dma((n_y - 1,)), dma((n_y - 1,)), dma((n_tp - 1,)), dma((n_tp - 1,)),
+        ],
+        compiler_params=pltpu.CompilerParams(collective_id=1, has_side_effects=True),
+        name="route",
+    )(ids_loc.reshape(1, tok), x_loc)
+
+
+def packed_kernel(
+    n_y, n_x, cap, table_ref, rows_hbm, wg_hbm, wu_hbm, wd_hbm, out_hbm,
+    x_buf, slot_buf, pair_buf, opp_buf, nbr_buf, w_in, w_out,
+    ys_send, ys_recv, ys_loc, a_send, a_recv, b_send, b_recv, d_send, d_recv,
+    p_send, p_recv, e_send, e_recv, n_send, n_recv, f_send, f_recv, h_send, h_recv, h_loc, w_sem,
+):
+    _, _, packed, d_model = x_buf.shape
+    n_loc = slot_buf.shape[0]
+    n_slots = n_loc * cap
+    hidden = w_out.shape[2]
+    half = packed // 2
+    n_src = 2 * n_x
+    n_grp = n_loc // GROUP
+    n_w = n_y * n_grp
+    yy = lax.axis_index("ep")
+    tt = lax.axis_index("tp")
+    xx, cc = tt // 2, tt % 2
+    xr, xl, xo = (xx + 1) % n_x, (xx + n_x - 1) % n_x, (xx + 2) % n_x
+    right, left, mate = {"tp": xr * 2 + cc}, {"tp": xl * 2 + cc}, {"tp": xx * 2 + 1 - cc}
+    sides = (right, left)
+    ahead, behind = (xr, xl), (xl, xr)
+    mine, other = cc * n_x, (1 - cc) * n_x
+
+    def remote(src, dst, send, recv, device):
+        return pltpu.make_async_remote_copy(
+            src_ref=src, dst_ref=dst, send_sem=send, recv_sem=recv, device_id=device, device_id_type=MESH
+        )
+
+    def part(h):
+        return pl.ds(h * half, half)
+
+    def y_copy(k):
+        q = n_y - k
+        peer = (yy + k) % n_y
+        return remote(rows_hbm.at[peer], x_buf.at[q, mine + xx], ys_send.at[q], ys_recv.at[q], {"ep": peer})
+
+    def y_local():
+        return pltpu.make_async_copy(rows_hbm.at[yy], x_buf.at[0, mine + xx], ys_loc)
+
+    def a_copy(t, k, h):
+        view = x_buf.at[t, mine + xx, part(h)]
+        return remote(view, view, a_send.at[t, k, h], a_recv.at[t, k, h], sides[k])
+
+    def a_arrival(t, k, h):
+        view = x_buf.at[t, mine + behind[k], part(h)]
+        return remote(view, view, a_send.at[t, k, h], a_recv.at[t, k, h], sides[k])
+
+    def b_copy(t, k):
+        view = x_buf.at[t, mine + behind[k], part(k)]
+        return remote(view, view, b_send.at[t, k], b_recv.at[t, k], sides[k])
+
+    def b_arrival(t, k):
+        view = x_buf.at[t, mine + xo, part(k)]
+        return remote(view, view, b_send.at[t, k], b_recv.at[t, k], sides[k])
+
+    def d_copy(t, k):
+        view = x_buf.at[t, mine + (xx, xl, xr, xo)[k]]
+        return remote(view, view, d_send.at[t, k], d_recv.at[t, k], mate)
+
+    def d_arrival(t, k):
+        view = x_buf.at[t, other + (xx, xl, xr, xo)[k]]
+        return remote(view, view, d_send.at[t, k], d_recv.at[t, k], mate)
+
+    def p_copy(t):
+        return remote(x_buf.at[t, pl.ds(other, n_x)], pair_buf.at[t], p_send.at[t], p_recv.at[t], mate)
+
+    def e_copy(t, k):
+        return remote(
+            x_buf.at[t, mine + xo, part(k)], opp_buf.at[k, t], e_send.at[t, k], e_recv.at[t, k], sides[k]
+        )
+
+    def n_copy(t, k):
+        h = 1 - k
+        return remote(
+            x_buf.at[t, mine + ahead[k], part(h)], nbr_buf.at[k, t, part(h)],
+            n_send.at[t, k], n_recv.at[t, k], sides[k],
+        )
+
+    def f_copy(t, k):
+        return remote(
+            x_buf.at[t, mine + ahead[k], part(k)], nbr_buf.at[k, t, part(k)],
+            f_send.at[t, k], f_recv.at[t, k], sides[k],
+        )
+
+    def h_copy(t):
+        return remote(x_buf.at[t, mine + xx], out_hbm.at[yy], h_send.at[t], h_recv.at[t], {"ep": (yy + t) % n_y})
+
+    def h_arrival(t):
+        return remote(
+            x_buf.at[t, mine + xx], out_hbm.at[(yy + n_y - t) % n_y], h_send.at[t], h_recv.at[t],
+            {"ep": (yy + t) % n_y},
+        )
+
+    def h_local():
+        return pltpu.make_async_copy(x_buf.at[0, mine + xx], out_hbm.at[yy], h_loc)
+
+    def w_copies(w):
+        s = w % W_SLOTS
+        at = pl.ds((w % n_grp) * GROUP, GROUP)
+        return (
+            pltpu.make_async_copy(wg_hbm.at[at], w_in.at[s, :, :, pl.ds(0, hidden)], w_sem.at[s, 0]),
+            pltpu.make_async_copy(wu_hbm.at[at], w_in.at[s, :, :, pl.ds(hidden, hidden)], w_sem.at[s, 1]),
+            pltpu.make_async_copy(wd_hbm.at[at], w_out.at[s], w_sem.at[s, 2]),
+        )
+
+    y_local().start()
+    for w in range(W_SLOTS):
+        for c in w_copies(w):
+            c.start()
+
+    barrier = pltpu.get_barrier_semaphore()
+    for device in [right, left, mate] + [{"ep": (yy + d) % n_y} for d in range(1, n_y)]:
+        pl.semaphore_signal(barrier, inc=1, device_id=device, device_id_type=MESH)
+    pl.semaphore_wait(barrier, 2 + n_y)
+
+    for k in range(n_y - 1, 0, -1):
+        y_copy(k).start()
+
+    def send_own(t):
+        for h in range(2):
+            for k in range(2):
+                a_copy(t, k, h if k == 0 else 1 - h).start()
+        d_copy(t, 0).start()
+
+    def pass_on(t):
+        for k in range(2):
+            a_arrival(t, k, k).wait_recv()
+            b_copy(t, k).start()
+
+    def share(t):
+        for k in range(2):
+            a_arrival(t, k, 1 - k).wait_recv()
+            d_copy(t, 1 + k).start()
+
+    def source_row(t, b):
+        row = table_ref[(b % n_x * 2 + b // n_x) * n_y + (yy + t) % n_y]
+        return row[:, :packed]
+
+    def spread(t):
+        @pl.loop(0, n_src)
+        def _(b):
+            to = source_row(t, b)
+            pick = (lax.broadcasted_iota(jnp.int32, (n_slots, packed), 0) == to).astype(F32).astype(BF16)
+            slots = jnp.dot(pick, x_buf[t, b], preferred_element_type=F32).astype(BF16)
+            slot_buf[:, b] = slots.reshape(n_loc, cap, d_model)
+
+    def multiply(t):
+        @pl.loop(0, n_grp)
+        def _(i):
+            w = t * n_grp + i
+            s = w % W_SLOTS
+            for c in w_copies(w):
+                c.wait()
+
+            @pl.loop(0, GROUP)
+            def _(el):
+                e = i * GROUP + el
+                tile = slot_buf[e].reshape(n_src * cap, d_model)
+                both = jnp.dot(tile, w_in[s, el], preferred_element_type=F32)
+                act = (jax.nn.silu(both[:, :hidden]) * both[:, hidden:]).astype(BF16)
+                out = jnp.dot(act, w_out[s, el], preferred_element_type=F32)
+                slot_buf[e] = out.astype(BF16).reshape(n_src, cap, d_model)
+
+            @pl.when(w + W_SLOTS < n_w)
+            def _():
+                for c in w_copies(w + W_SLOTS):
+                    c.start()
+
+    def gather_back(t, base):
+        @pl.loop(0, n_x)
+        def _(j):
+            b = base + j
+            to = source_row(t, b).astype(F32)
+            col = jnp.transpose(jnp.broadcast_to(to, (128, packed)))
+            lane = lax.broadcasted_iota(jnp.int32, (packed, 128), 1).astype(F32)
+            pick = jnp.concatenate(
+                [(col == lane + float(128 * m)).astype(F32).astype(BF16) for m in range(n_slots // 128)], axis=1
+            )
+            slots = slot_buf[:, b].reshape(n_slots, d_model)
+            x_buf[t, b] = jnp.dot(pick, slots, preferred_element_type=F32).astype(BF16)
+
+    def pair_sum(t, blk, h, extra=None):
+        total = x_buf[t, mine + blk, h * half:(h + 1) * half].astype(F32)
+        total = total + pair_buf[t, blk, h * half:(h + 1) * half].astype(F32)
+        if extra is not None:
+            total = total + extra.astype(F32)
+        x_buf[t, mine + blk, h * half:(h + 1) * half] = total.astype(BF16)
+
+    def first_sums(t):
+        p_copy(t).wait_recv()
+        for k in range(2):
+            pair_sum(t, xo, k)
+            e_copy(t, k).start()
+        for k in range(2):
+            pair_sum(t, ahead[k], 1 - k)
+            n_copy(t, k).start()
+
+    def last_sums(t):
+        for k in range(2):
+            e_copy(t, k).wait_recv()
+            pair_sum(t, ahead[k], k, opp_buf[k, t])
+            f_copy(t, k).start()
+
+    def give_back(t):
+        for k in range(2):
+            n_copy(t, k).wait_recv()
+            f_copy(t, k).wait_recv()
+        for h in range(2):
+            at = slice(h * half, (h + 1) * half)
+            pair_sum(t, xx, h, nbr_buf[0, t, at].astype(F32) + nbr_buf[1, t, at].astype(F32))
+
+        @pl.when(t == 0)
+        def _():
+            h_local().start()
+
+        @pl.when(t > 0)
+        def _():
+            h_copy(t).start()
+
+    def own_rows(t):
+        y_copy(n_y - t).wait_recv()
+
+    y_local().wait()
+    send_own(0)
+    pass_on(0)
+    own_rows(1)
+    send_own(1)
+    share(0)
+
+    @pl.loop(0, n_y)
+    def _(t):
+        for k in range(2):
+            b_arrival(t, k).wait_recv()
+        d_copy(t, 3).start()
+        for k in range(4):
+            d_arrival(t, k).wait_recv()
+        spread(t)
+
+        @pl.when(t + 1 < n_y)
+        def _():
+            pass_on(t + 1)
+
+        @pl.when(t + 2 < n_y)
+        def _():
+            own_rows(t + 2)
+            send_own(t + 2)
+
+        multiply(t)
+
+        @pl.when(t + 1 < n_y)
+        def _():
+            share(t + 1)
+
+        @pl.when(t > 0)
+        def _():
+            last_sums(t - 1)
+
+        for k in range(2):
+            for h in range(2):
+                a_copy(t, k, h).wait_send()
+            b_copy(t, k).wait_send()
+        for k in range(4):
+            d_copy(t, k).wait_send()
+        gather_back(t, other)
+        p_copy(t).start()
+        gather_back(t, mine)
+        first_sums(t)
+
+        @pl.when(t > 1)
+        def _():
+            give_back(t - 2)
+
+    last_sums(n_y - 1)
+    give_back(n_y - 2)
+    give_back(n_y - 1)
+
+    for k in range(1, n_y):
+        y_copy(k).wait_send()
+        h_copy(k).wait_send()
+        h_arrival(k).wait_recv()
+    h_local().wait()
+
+    @pl.loop(0, n_y)
+    def _(t):
+        p_copy(t).wait_send()
+        for k in range(2):
+            e_copy(t, k).wait_send()
+            n_copy(t, k).wait_send()
+            f_copy(t, k).wait_send()
+
+
+def packed_experts(table, rows, wg, wu, wd, n_tp, cap):
+    n_y, packed, d_model = rows.shape
+    n_loc, _, hidden = wg.shape
+    n_x = n_tp // 2
+    half = packed // 2
+    dma = pltpu.SemaphoreType.DMA
+    hbm = pl.BlockSpec(memory_space=pltpu.HBM)
+    return pl.pallas_call(
+        functools.partial(packed_kernel, n_y, n_x, cap),
+        out_shape=jax.ShapeDtypeStruct(rows.shape, BF16),
+        in_specs=[pl.BlockSpec(memory_space=pltpu.VMEM)] + [hbm] * 4,
+        out_specs=hbm,
+        scratch_shapes=[
+            pltpu.VMEM((n_y, 2 * n_x, packed, d_model), BF16),
+            pltpu.VMEM((n_loc, 2 * n_x, cap, d_model), BF16),
+            pltpu.VMEM((n_y, n_x, packed, d_model), BF16),
+            pltpu.VMEM((2, n_y, half, d_model), BF16),
+            pltpu.VMEM((2, n_y, packed, d_model), BF16),
+            pltpu.VMEM((W_SLOTS, GROUP, d_model, 2 * hidden), BF16),
+            pltpu.VMEM((W_SLOTS, GROUP, hidden, d_model), BF16),
+            dma((n_y,)), dma((n_y,)), dma,
+            dma((n_y, 2, 2)), dma((n_y, 2, 2)),
+            dma((n_y, 2)), dma((n_y, 2)),
+            dma((n_y, 4)), dma((n_y, 4)),
+            dma((n_y,)), dma((n_y,)),
+            dma((n_y, 2)), dma((n_y, 2)),
+            dma((n_y, 2)), dma((n_y, 2)),
+            dma((n_y, 2)), dma((n_y, 2)),
+            dma((n_y,)), dma((n_y,)), dma,
+            dma((W_SLOTS, 3)),
+        ],
+        compiler_params=pltpu.CompilerParams(
+            collective_id=2, has_side_effects=True, vmem_limit_bytes=67043328
+        ),
+        name="packed_experts",
+    )(table, rows, wg, wu, wd)
+
+
 def solution(mesh):
     n_y, n_tp = mesh.shape["ep"], mesh.shape["tp"]
     row_spec = P(("dp", "ep", "tp"), None)
 
     def local_layer(x_loc, ids_loc, gate_loc, wg_loc, wu_loc, wd_loc):
         tok, d_model = x_loc.shape
-        n_exp = wg_loc.shape[0] * n_y
+        n_loc = wg_loc.shape[0]
+        n_exp = n_loc * n_y
         capacity = CAP_FACTOR * tok // n_exp
-        rows, pos = dispatch(x_loc, ids_loc, n_exp, capacity)
-        y = experts(rows.reshape(n_exp, capacity, d_model), wg_loc, wu_loc, wd_loc, n_y, n_tp)
-        return combine(pos, gate_loc, y.reshape(n_exp * capacity, d_model))
+        packed = n_loc * capacity * 5 // 8
+        rows, pos, table, most = route(x_loc, ids_loc, n_exp, capacity, packed, n_y, n_tp)
+
+        def by_rows():
+            y = packed_experts(table, rows, wg_loc, wu_loc, wd_loc, n_tp, capacity)
+            return combine(pos, gate_loc, y.reshape(n_y * packed, d_model))
+
+        def by_slots():
+            rows, pos = dispatch(x_loc, ids_loc, n_exp, capacity)
+            y = experts(rows.reshape(n_exp, capacity, d_model), wg_loc, wu_loc, wd_loc, n_y, n_tp)
+            return combine(pos, gate_loc, y.reshape(n_exp * capacity, d_model))
+
+        return lax.cond(most[0, 0] <= packed, by_rows, by_slots)
 
     return jax.shard_map(local_layer, mesh=mesh, in_specs=(row_spec, row_spec, row_spec, P("ep", None, "tp"), P("ep", None, "tp"), P("ep", "tp", None)), out_specs=row_spec, check_vma=False)

time: 244 us -> 190 us (0.78)
  Pallas kernels: 239 us -> 184 us
    pallas_call x2, Pallas kernels: 232 us -> 179 us  [the longest x1 162 us: packed_experts(): pl.pallas_call(functools.partial(packed_kernel, n_y, n_x, cap), out_shape...]
    pallas_call x1, Pallas kernels: 7.48 us -> 4.97 us  [combine(): pl.pallas_call(combine_kernel, out_shape=jax.ShapeDtypeStruct((tok, y_slo...]
where the time goes in v2:
time: 190 us; the launch traced here: 189 us
  Pallas kernels  184 us (97%)
  local copies, waits for them, and re-layouts  4.55 us (2%)
    pallas_call x1, Pallas kernels, packed_experts(): pl.pallas_call(functools.partial(packed_kernel, n_y, n_x, cap), out_shape...  162 us
    pallas_call x1, Pallas kernels, route(): pl.pallas_call(functools.partial(route_kernel, n_y, n_tp, n_exp, capacity...  17.3 us
    pallas_call x1, Pallas kernels, combine(): pl.pallas_call(combine_kernel, out_shape=jax.ShapeDtypeStruct((tok, y_slo...  4.97 us

profile of v2, /device:TPU:97, one launch (start us, length us, event | category | flops | bytes accessed | tf_op | source)
XLA Modules:
  0.0 189.4 jit_solution(910674197867297490)
XLA Ops:
  0.0 17.3 %route.1 = (bf16[4,320,768]{2,1,0:T(8,128)(2,1)}, s32[1,1024]{1,0:T(1,128)}, s32[32,1,384]{2,1,0:T(1,128)}, s32[1,64]{1,0:T(1,128)}) custom-call(s32[1,1024]{1,0:T(1,128)} %bitcast.12, bf16[1024,768]{1,0:T(8,128)(2,1)} %x_ref.1), custom_call_target="tpu_custom_call" | custom-call | tf_op jit(solution)/shard_map/route/pallas_call | solution.py:429
  17.9 170.4 %conditional.1 = (bf16[1024,768]{1,0:T(8,128)(2,1)S(1)}) conditional(s32[]{:T(128)} %bitcast.7, (s32[1024,1]{0,1:T(1,128)}, bf16[1024,768]{1,0:T(8,128)(2,1)}, bf16[16,768,384]{2,1,0:T(8,128)(2,1)}, bf16[16,768,384]{2,1,0:T(8,128)(2,1)}, bf16[16,384,768]{2,1,0:T(8,128)(2,1)}, /*index=5*/f32[1024,1]{0,1:T(1,128)}) %tuple.11, (s32[1,1024]{1,0:T(1,128)}, ...), branch_computations={%region_0.0_spmd, %region_1.0_spmd} | conditional | bytes 16392 | solution.py:796
  17.9 162.0 %packed_experts.1 = bf16[4,320,768]{2,1,0:T(8,128)(2,1)} custom-call(s32[32,1,384]{2,1,0:T(1,128)} %get-tuple-element.44.table_ref, bf16[4,320,768]{2,1,0:T(8,128)(2,1)} %get-tuple-element.45.rows_hbm, bf16[16,768,384]{2,1,0:T(8,128)(2,1)} %get-tuple-element.46.wg_hbm, bf16[16,768,384]{2,1,0:T(8,128)(2,1)} %get-tuple-element.47.wu_hbm, ...), custom_call_target="tpu_custom_call" | custom-call | tf_op jit(solution)/shard_map/cond/branch_1_fun/packed_experts/pallas_call | solution.py:744
  179.9 1.7 copy.12.pos_ref
  181.6 1.7 copy.14.gate_ref
  183.3 5.0 %combine.3 = bf16[1024,768]{1,0:T(8,128)(2,1)S(1)} custom-call(s32[1024,1]{1,0:T(8,128)} %copy.12.pos_ref, f32[1024,1]{1,0:T(8,128)} %copy.14.gate_ref, bf16[1280,768]{1,0:T(8,128)(2,1)} %bitcast.10), custom_call_target="tpu_custom_call" | custom-call | tf_op jit(solution)/shard_map/cond/branch_1_fun/combine/pallas_call | solution.py:67
  188.3 0.0 copy-start
  188.3 1.1 copy-done
Async XLA Ops:
  188.3 1.1 copy-start

commit v3 on v2

--- a/solution.py
+++ b/solution.py
@@ -324,11 +324,10 @@
 
 
 def route_kernel(
-    n_y, n_tp, n_exp, capacity, ids_ref, x_ref, rows_ref, pos_ref, table_ref, most_ref,
+    n_y, n_tp, n_exp, capacity, packed, ids_ref, pos_ref, table_ref, most_ref,
     meta, col_send, col_recv, row_send, row_recv,
 ):
     tok = ids_ref.shape[1]
-    packed = rows_ref.shape[1]
     width = table_ref.shape[2]
     n_loc = n_exp // n_y
     yy = lax.axis_index("ep")
@@ -355,18 +354,17 @@
     counts = jnp.sum(to_rank.astype(F32), axis=1, keepdims=True)
     most = jnp.max(counts, axis=0, keepdims=True).astype(jnp.int32)
     fits = kept & (place < packed)
-    pos_ref[...] = jnp.where(fits, rank * packed + place, -1)
-    key = jnp.where(fits, rank * tok + place, -1)
+    pos = jnp.where(fits, rank * packed + place, -1)
+    pos_ref[...] = pos
     row_id = lax.broadcasted_iota(jnp.int32, (pad, tok), 0)
     parts = jnp.where(row_id == 0, (ids % n_loc).astype(F32), jnp.where(row_id == 1, slot, 1.0))
     parts = jnp.where(kept, parts, 0.0).astype(BF16)
 
-    def pick(r):
-        return ((lax.broadcasted_iota(jnp.int32, (packed, tok), 0) + r * tok) == key).astype(F32).astype(BF16)
-
     @pl.loop(0, n_y)
     def _(r):
-        got = lax.dot_general(parts, pick(r), (((1,), (1,)), ((), ())), preferred_element_type=F32)
+        pick = (lax.broadcasted_iota(jnp.int32, (packed, tok), 0) + r * packed) == pos
+        pick = pick.astype(F32).astype(BF16)
+        got = lax.dot_general(parts, pick, (((1,), (1,)), ((), ())), preferred_element_type=F32)
         where = jnp.where(got[2:3] > 0.5, got[0:1] * capacity + got[1:2], -1.0)
         meta[r, :, 0:packed] = where.astype(jnp.int32)
         meta[r, :, packed:width] = jnp.broadcast_to(most, (1, width - packed))
@@ -404,11 +402,6 @@
 
     for k in range(len(y_peers)):
         col_copy(k).start()
-
-    @pl.loop(0, n_y)
-    def _(r):
-        rows_ref[r] = jnp.dot(pick(r), x_ref[...], preferred_element_type=F32).astype(BF16)
-
     for k in range(len(y_peers)):
         col_arrival(k).wait_recv()
     for k in range(len(t_peers)):
@@ -422,14 +415,13 @@
         row_copy(k).wait_send()
 
 
-def route(x_loc, ids_loc, n_exp, capacity, packed, n_y, n_tp):
-    tok, d_model = x_loc.shape
+def route(ids_loc, n_exp, capacity, packed, n_y, n_tp):
+    tok = ids_loc.shape[0]
     width = -(-(packed + 1) // 128) * 128
     dma = pltpu.SemaphoreType.DMA
     return pl.pallas_call(
-        functools.partial(route_kernel, n_y, n_tp, n_exp, capacity),
+        functools.partial(route_kernel, n_y, n_tp, n_exp, capacity, packed),
         out_shape=(
-            jax.ShapeDtypeStruct((n_y, packed, d_model), BF16),
             jax.ShapeDtypeStruct((1, tok), jnp.int32),
             jax.ShapeDtypeStruct((n_y * n_tp, 1, width), jnp.int32),
             jax.ShapeDtypeStruct((1, width - packed), jnp.int32),
@@ -440,17 +432,17 @@
         ],
         compiler_params=pltpu.CompilerParams(collective_id=1, has_side_effects=True),
         name="route",
-    )(ids_loc.reshape(1, tok), x_loc)
+    )(ids_loc.reshape(1, tok))
 
 
 def packed_kernel(
-    n_y, n_x, cap, table_ref, rows_hbm, wg_hbm, wu_hbm, wd_hbm, out_hbm,
-    x_buf, slot_buf, pair_buf, opp_buf, nbr_buf, w_in, w_out,
-    ys_send, ys_recv, ys_loc, a_send, a_recv, b_send, b_recv, d_send, d_recv,
-    p_send, p_recv, e_send, e_recv, n_send, n_recv, f_send, f_recv, h_send, h_recv, h_loc, w_sem,
+    n_y, n_x, packed, cap, pos_ref, gate_ref, table_ref, x_ref, wg_hbm, wu_hbm, wd_hbm, out_ref,
+    pack_buf, x_buf, slot_buf, pair_buf, opp_buf, nbr_buf, ret_buf, w_in, w_out, pos_col, gate_col,
+    ys_send, ys_recv, a_send, a_recv, b_send, b_recv, s_send, s_recv,
+    p_send, p_recv, e_send, e_recv, n_send, n_recv, f_send, f_recv, h_send, h_recv, w_sem,
 ):
-    _, _, packed, d_model = x_buf.shape
-    n_loc = slot_buf.shape[0]
+    tok, d_model = x_ref.shape
+    n_loc = slot_buf.shape[1]
     n_slots = n_loc * cap
     hidden = w_out.shape[2]
     half = packed // 2
@@ -466,6 +458,12 @@
     ahead, behind = (xr, xl), (xl, xr)
     mine, other = cc * n_x, (1 - cc) * n_x
 
+    def row_of(t):
+        return (yy + t + cc * (n_y - 2 * t) + n_y) % n_y
+
+    def row_to(t):
+        return (yy - t - cc * (n_y - 2 * t) + 2 * n_y) % n_y
+
     def remote(src, dst, send, recv, device):
         return pltpu.make_async_remote_copy(
             src_ref=src, dst_ref=dst, send_sem=send, recv_sem=recv, device_id=device, device_id_type=MESH
@@ -474,70 +472,55 @@
     def part(h):
         return pl.ds(h * half, half)
 
-    def y_copy(k):
-        q = n_y - k
-        peer = (yy + k) % n_y
-        return remote(rows_hbm.at[peer], x_buf.at[q, mine + xx], ys_send.at[q], ys_recv.at[q], {"ep": peer})
-
-    def y_local():
-        return pltpu.make_async_copy(rows_hbm.at[yy], x_buf.at[0, mine + xx], ys_loc)
+    def y_copy(t):
+        return remote(pack_buf.at[t], x_buf.at[t, xx], ys_send.at[t], ys_recv.at[t], {"ep": row_to(t)})
 
     def a_copy(t, k, h):
-        view = x_buf.at[t, mine + xx, part(h)]
+        view = x_buf.at[t, xx, part(h)]
         return remote(view, view, a_send.at[t, k, h], a_recv.at[t, k, h], sides[k])
 
     def a_arrival(t, k, h):
-        view = x_buf.at[t, mine + behind[k], part(h)]
+        view = x_buf.at[t, behind[k], part(h)]
         return remote(view, view, a_send.at[t, k, h], a_recv.at[t, k, h], sides[k])
 
     def b_copy(t, k):
-        view = x_buf.at[t, mine + behind[k], part(k)]
+        view = x_buf.at[t, behind[k], part(k)]
         return remote(view, view, b_send.at[t, k], b_recv.at[t, k], sides[k])
 
     def b_arrival(t, k):
-        view = x_buf.at[t, mine + xo, part(k)]
+        view = x_buf.at[t, xo, part(k)]
         return remote(view, view, b_send.at[t, k], b_recv.at[t, k], sides[k])
 
-    def d_copy(t, k):
-        view = x_buf.at[t, mine + (xx, xl, xr, xo)[k]]
-        return remote(view, view, d_send.at[t, k], d_recv.at[t, k], mate)
-
-    def d_arrival(t, k):
-        view = x_buf.at[t, other + (xx, xl, xr, xo)[k]]
-        return remote(view, view, d_send.at[t, k], d_recv.at[t, k], mate)
-
-    def p_copy(t):
-        return remote(x_buf.at[t, pl.ds(other, n_x)], pair_buf.at[t], p_send.at[t], p_recv.at[t], mate)
+    def s_copy(t, b):
+        view = slot_buf.at[t % 2, :, mine + b]
+        return remote(view, view, s_send.at[t, b], s_recv.at[t, b], mate)
+
+    def s_arrival(t, b):
+        view = slot_buf.at[t % 2, :, other + b]
+        return remote(view, view, s_send.at[t, b], s_recv.at[t, b], mate)
+
+    def p_copy(t, i):
+        at = pl.ds(i * GROUP, GROUP)
+        return remote(
+            slot_buf.at[t % 2, at, pl.ds(other, n_x)], pair_buf.at[t % 2, at], p_send.at[t, i], p_recv.at[t, i], mate
+        )
 
     def e_copy(t, k):
-        return remote(
-            x_buf.at[t, mine + xo, part(k)], opp_buf.at[k, t], e_send.at[t, k], e_recv.at[t, k], sides[k]
-        )
+        return remote(x_buf.at[t, xo, part(k)], opp_buf.at[k, t], e_send.at[t, k], e_recv.at[t, k], sides[k])
 
     def n_copy(t, k):
         h = 1 - k
         return remote(
-            x_buf.at[t, mine + ahead[k], part(h)], nbr_buf.at[k, t, part(h)],
-            n_send.at[t, k], n_recv.at[t, k], sides[k],
+            x_buf.at[t, ahead[k], part(h)], nbr_buf.at[k, t, part(h)], n_send.at[t, k], n_recv.at[t, k], sides[k]
         )
 
     def f_copy(t, k):
         return remote(
-            x_buf.at[t, mine + ahead[k], part(k)], nbr_buf.at[k, t, part(k)],
-            f_send.at[t, k], f_recv.at[t, k], sides[k],
+            x_buf.at[t, ahead[k], part(k)], nbr_buf.at[k, t, part(k)], f_send.at[t, k], f_recv.at[t, k], sides[k]
         )
 
     def h_copy(t):
-        return remote(x_buf.at[t, mine + xx], out_hbm.at[yy], h_send.at[t], h_recv.at[t], {"ep": (yy + t) % n_y})
-
-    def h_arrival(t):
-        return remote(
-            x_buf.at[t, mine + xx], out_hbm.at[(yy + n_y - t) % n_y], h_send.at[t], h_recv.at[t],
-            {"ep": (yy + t) % n_y},
-        )
-
-    def h_local():
-        return pltpu.make_async_copy(x_buf.at[0, mine + xx], out_hbm.at[yy], h_loc)
+        return remote(x_buf.at[t, xx], ret_buf.at[t], h_send.at[t], h_recv.at[t], {"ep": row_of(t)})
 
     def w_copies(w):
         s = w % W_SLOTS
@@ -548,138 +531,166 @@
             pltpu.make_async_copy(wd_hbm.at[at], w_out.at[s], w_sem.at[s, 2]),
         )
 
-    y_local().start()
-    for w in range(W_SLOTS):
-        for c in w_copies(w):
-            c.start()
-
     barrier = pltpu.get_barrier_semaphore()
     for device in [right, left, mate] + [{"ep": (yy + d) % n_y} for d in range(1, n_y)]:
         pl.semaphore_signal(barrier, inc=1, device_id=device, device_id_type=MESH)
-    pl.semaphore_wait(barrier, 2 + n_y)
-
-    for k in range(n_y - 1, 0, -1):
-        y_copy(k).start()
+
+    def pack(t):
+        first = row_to(t) * packed
+        pick = (lax.broadcasted_iota(jnp.int32, (packed, tok), 0) + first) == pos_ref[...]
+        return jnp.dot(pick.astype(F32).astype(BF16), x_ref[...], preferred_element_type=F32).astype(BF16)
 
     def send_own(t):
         for h in range(2):
             for k in range(2):
                 a_copy(t, k, h if k == 0 else 1 - h).start()
-        d_copy(t, 0).start()
 
     def pass_on(t):
         for k in range(2):
             a_arrival(t, k, k).wait_recv()
             b_copy(t, k).start()
 
-    def share(t):
-        for k in range(2):
-            a_arrival(t, k, 1 - k).wait_recv()
-            d_copy(t, 1 + k).start()
-
     def source_row(t, b):
-        row = table_ref[(b % n_x * 2 + b // n_x) * n_y + (yy + t) % n_y]
+        row = table_ref[(b * 2 + cc) * n_y + row_of(t)]
         return row[:, :packed]
 
-    def spread(t):
-        @pl.loop(0, n_src)
-        def _(b):
+    def spread(t, blocks):
+        @pl.loop(0, len(blocks))
+        def _(j):
+            b = blocks[0]
+            for n, blk in enumerate(blocks[1:]):
+                b = jnp.where(j == n + 1, blk, b)
             to = source_row(t, b)
             pick = (lax.broadcasted_iota(jnp.int32, (n_slots, packed), 0) == to).astype(F32).astype(BF16)
             slots = jnp.dot(pick, x_buf[t, b], preferred_element_type=F32).astype(BF16)
-            slot_buf[:, b] = slots.reshape(n_loc, cap, d_model)
-
-    def multiply(t):
-        @pl.loop(0, n_grp)
+            slot_buf[t % 2, :, mine + b] = slots.reshape(n_loc, cap, d_model)
+            s_copy(t, b).start()
+
+    def share(t):
+        for k in range(2):
+            a_arrival(t, k, 1 - k).wait_recv()
+        spread(t, (xl, xr))
+
+    def multiply(t, lo, hi):
+        @pl.loop(lo, hi)
         def _(i):
             w = t * n_grp + i
             s = w % W_SLOTS
             for c in w_copies(w):
                 c.wait()
-
-            @pl.loop(0, GROUP)
-            def _(el):
-                e = i * GROUP + el
-                tile = slot_buf[e].reshape(n_src * cap, d_model)
-                both = jnp.dot(tile, w_in[s, el], preferred_element_type=F32)
-                act = (jax.nn.silu(both[:, :hidden]) * both[:, hidden:]).astype(BF16)
+            both = []
+            for el in range(GROUP):
+                tile = slot_buf[t % 2, i * GROUP + el].reshape(n_src * cap, d_model)
+                both.append(jnp.dot(tile, w_in[s, el], preferred_element_type=F32))
+            for el in range(GROUP):
+                act = (jax.nn.silu(both[el][:, :hidden]) * both[el][:, hidden:]).astype(BF16)
                 out = jnp.dot(act, w_out[s, el], preferred_element_type=F32)
-                slot_buf[e] = out.astype(BF16).reshape(n_src, cap, d_model)
+                slot_buf[t % 2, i * GROUP + el] = out.astype(BF16).reshape(n_src, cap, d_model)
+            p_copy(t, i).start()
 
             @pl.when(w + W_SLOTS < n_w)
             def _():
                 for c in w_copies(w + W_SLOTS):
                     c.start()
 
-    def gather_back(t, base):
-        @pl.loop(0, n_x)
+    def gather_back(t, blocks):
+        @pl.loop(0, len(blocks))
         def _(j):
-            b = base + j
+            b = blocks[0]
+            for n, blk in enumerate(blocks[1:]):
+                b = jnp.where(j == n + 1, blk, b)
             to = source_row(t, b).astype(F32)
             col = jnp.transpose(jnp.broadcast_to(to, (128, packed)))
             lane = lax.broadcasted_iota(jnp.int32, (packed, 128), 1).astype(F32)
             pick = jnp.concatenate(
                 [(col == lane + float(128 * m)).astype(F32).astype(BF16) for m in range(n_slots // 128)], axis=1
             )
-            slots = slot_buf[:, b].reshape(n_slots, d_model)
+            total = slot_buf[t % 2, :, mine + b].astype(F32) + pair_buf[t % 2, :, b].astype(F32)
+            slots = total.astype(BF16).reshape(n_slots, d_model)
             x_buf[t, b] = jnp.dot(pick, slots, preferred_element_type=F32).astype(BF16)
 
-    def pair_sum(t, blk, h, extra=None):
-        total = x_buf[t, mine + blk, h * half:(h + 1) * half].astype(F32)
-        total = total + pair_buf[t, blk, h * half:(h + 1) * half].astype(F32)
-        if extra is not None:
-            total = total + extra.astype(F32)
-        x_buf[t, mine + blk, h * half:(h + 1) * half] = total.astype(BF16)
-
     def first_sums(t):
-        p_copy(t).wait_recv()
-        for k in range(2):
-            pair_sum(t, xo, k)
+        @pl.loop(0, n_grp)
+        def _(i):
+            p_copy(t, i).wait_recv()
+
+        gather_back(t, (xo,))
+        for k in range(2):
             e_copy(t, k).start()
-        for k in range(2):
-            pair_sum(t, ahead[k], 1 - k)
+        gather_back(t, (xr, xl))
+        for k in range(2):
             n_copy(t, k).start()
 
     def last_sums(t):
         for k in range(2):
             e_copy(t, k).wait_recv()
-            pair_sum(t, ahead[k], k, opp_buf[k, t])
+            at = (t, ahead[k], slice(k * half, (k + 1) * half))
+            x_buf[at] = (x_buf[at].astype(F32) + opp_buf[k, t].astype(F32)).astype(BF16)
             f_copy(t, k).start()
 
-    def give_back(t):
+    def give_back(t, local):
         for k in range(2):
             n_copy(t, k).wait_recv()
             f_copy(t, k).wait_recv()
-        for h in range(2):
-            at = slice(h * half, (h + 1) * half)
-            pair_sum(t, xx, h, nbr_buf[0, t, at].astype(F32) + nbr_buf[1, t, at].astype(F32))
-
-        @pl.when(t == 0)
-        def _():
-            h_local().start()
-
-        @pl.when(t > 0)
-        def _():
+        total = x_buf[t, xx].astype(F32) + (nbr_buf[0, t].astype(F32) + nbr_buf[1, t].astype(F32))
+        if local:
+            ret_buf[t] = total.astype(BF16)
+        else:
+            x_buf[t, xx] = total.astype(BF16)
             h_copy(t).start()
 
-    def own_rows(t):
-        y_copy(n_y - t).wait_recv()
-
-    y_local().wait()
+    def combine_into(t, first, last):
+        if not isinstance(t, int) or t > 0:
+            h_copy(t).wait_recv()
+        tile = 256
+
+        @pl.loop(0, tok // tile)
+        def _(i):
+            rows = pl.ds(pl.multiple_of(i * tile, tile), tile)
+            want = pos_col[rows, :] - (row_to(t) * packed).astype(F32)
+            lane = lax.broadcasted_iota(jnp.int32, (tile, 128), 1).astype(F32)
+            pick = jnp.concatenate(
+                [(want == lane + float(128 * m)).astype(F32) for m in range(-(-packed // 128))], axis=1
+            )
+            y = jnp.dot(pick[:, :packed].astype(BF16), ret_buf[t], preferred_element_type=F32)
+            if not first:
+                y = y + out_ref[rows, :].astype(F32)
+            if last:
+                weight = jnp.where(pos_col[rows, 0:1] >= 0, gate_col[rows, 0:1], 0.0)
+                y = y * weight
+            out_ref[rows, :] = y.astype(BF16)
+
+    x_buf[0, xx] = pack(0)
+    pl.semaphore_wait(barrier, 2 + n_y)
     send_own(0)
+
+    @pl.loop(1, n_y)
+    def _(t):
+        pack_buf[t] = pack(t)
+        y_copy(t).start()
+
+    for w in range(W_SLOTS):
+        for c in w_copies(w):
+            c.start()
+    spread(0, (xx,))
     pass_on(0)
-    own_rows(1)
+    y_copy(1).wait_recv()
     send_own(1)
+    tile = 256
+
+    @pl.loop(0, tok // tile)
+    def _(i):
+        rows = pl.ds(pl.multiple_of(i * tile, tile), tile)
+        pos_col[rows, :] = jnp.transpose(jnp.broadcast_to(pos_ref[:, rows].astype(F32), (128, tile)))
+        gate_col[rows, :] = jnp.transpose(jnp.broadcast_to(gate_ref[:, rows], (128, tile)))
+
     share(0)
 
     @pl.loop(0, n_y)
     def _(t):
         for k in range(2):
             b_arrival(t, k).wait_recv()
-        d_copy(t, 3).start()
-        for k in range(4):
-            d_arrival(t, k).wait_recv()
-        spread(t)
+        spread(t, (xo,))
 
         @pl.when(t + 1 < n_y)
         def _():
@@ -687,89 +698,108 @@
 
         @pl.when(t + 2 < n_y)
         def _():
-            own_rows(t + 2)
+            y_copy(t + 2).wait_recv()
             send_own(t + 2)
 
-        multiply(t)
+        for b in range(n_x):
+            s_arrival(t, b).wait_recv()
+            s_copy(t, b).wait_send()
+        multiply(t, 0, n_grp // 2)
+
+        @pl.when(t + 1 < n_y)
+        def _():
+            spread(t + 1, (xx,))
+
+        multiply(t, n_grp // 2, n_grp)
+
+        @pl.when(t > 0)
+        def _():
+            last_sums(t - 1)
 
         @pl.when(t + 1 < n_y)
         def _():
             share(t + 1)
 
-        @pl.when(t > 0)
-        def _():
-            last_sums(t - 1)
-
         for k in range(2):
             for h in range(2):
                 a_copy(t, k, h).wait_send()
             b_copy(t, k).wait_send()
-        for k in range(4):
-            d_copy(t, k).wait_send()
-        gather_back(t, other)
-        p_copy(t).start()
-        gather_back(t, mine)
         first_sums(t)
-
-        @pl.when(t > 1)
+        gather_back(t, (xx,))
+
+        @pl.loop(0, n_grp)
+        def _(i):
+            p_copy(t, i).wait_send()
+
+        @pl.when(t == 2)
         def _():
-            give_back(t - 2)
+            give_back(0, True)
+
+        @pl.when(t > 2)
+        def _():
+            give_back(t - 2, False)
 
     last_sums(n_y - 1)
-    give_back(n_y - 2)
-    give_back(n_y - 1)
-
-    for k in range(1, n_y):
-        y_copy(k).wait_send()
-        h_copy(k).wait_send()
-        h_arrival(k).wait_recv()
-    h_local().wait()
+    for t in range(max(n_y - 2, 0), n_y):
+        if t == n_y - 1:
+            combine_into(0, True, False)
+        give_back(t, t == 0)
+    for t in range(1, n_y):
+        combine_into(t, False, t == n_y - 1)
+    for t in range(1, n_y):
+        y_copy(t).wait_send()
+        h_copy(t).wait_send()
 
     @pl.loop(0, n_y)
     def _(t):
-        p_copy(t).wait_send()
         for k in range(2):
             e_copy(t, k).wait_send()
             n_copy(t, k).wait_send()
             f_copy(t, k).wait_send()
 
 
-def packed_experts(table, rows, wg, wu, wd, n_tp, cap):
-    n_y, packed, d_model = rows.shape
+def packed_layer(pos, gate, table, x_loc, wg, wu, wd, n_y, n_tp, packed, cap):
+    tok, d_model = x_loc.shape
     n_loc, _, hidden = wg.shape
     n_x = n_tp // 2
+    n_grp = n_loc // GROUP
     half = packed // 2
     dma = pltpu.SemaphoreType.DMA
     hbm = pl.BlockSpec(memory_space=pltpu.HBM)
+    vmem = pl.BlockSpec(memory_space=pltpu.VMEM)
     return pl.pallas_call(
-        functools.partial(packed_kernel, n_y, n_x, cap),
-        out_shape=jax.ShapeDtypeStruct(rows.shape, BF16),
-        in_specs=[pl.BlockSpec(memory_space=pltpu.VMEM)] + [hbm] * 4,
-        out_specs=hbm,
+        functools.partial(packed_kernel, n_y, n_x, packed, cap),
+        out_shape=jax.ShapeDtypeStruct((tok, d_model), BF16),
+        in_specs=[vmem] * 4 + [hbm] * 3,
+        out_specs=vmem,
         scratch_shapes=[
-            pltpu.VMEM((n_y, 2 * n_x, packed, d_model), BF16),
-            pltpu.VMEM((n_loc, 2 * n_x, cap, d_model), BF16),
+            pltpu.VMEM((n_y, packed, d_model), BF16),
             pltpu.VMEM((n_y, n_x, packed, d_model), BF16),
+            pltpu.VMEM((2, n_loc, 2 * n_x, cap, d_model), BF16),
+            pltpu.VMEM((2, n_loc, n_x, cap, d_model), BF16),
             pltpu.VMEM((2, n_y, half, d_model), BF16),
             pltpu.VMEM((2, n_y, packed, d_model), BF16),
+            pltpu.VMEM((n_y, packed, d_model), BF16),
             pltpu.VMEM((W_SLOTS, GROUP, d_model, 2 * hidden), BF16),
             pltpu.VMEM((W_SLOTS, GROUP, hidden, d_model), BF16),
-            dma((n_y,)), dma((n_y,)), dma,
+            pltpu.VMEM((tok, 128), F32),
+            pltpu.VMEM((tok, 128), F32),
+            dma((n_y,)), dma((n_y,)),
             dma((n_y, 2, 2)), dma((n_y, 2, 2)),
             dma((n_y, 2)), dma((n_y, 2)),
-            dma((n_y, 4)), dma((n_y, 4)),
-            dma((n_y,)), dma((n_y,)),
+            dma((n_y, n_x)), dma((n_y, n_x)),
+            dma((n_y, n_grp)), dma((n_y, n_grp)),
             dma((n_y, 2)), dma((n_y, 2)),
             dma((n_y, 2)), dma((n_y, 2)),
             dma((n_y, 2)), dma((n_y, 2)),
-            dma((n_y,)), dma((n_y,)), dma,
+            dma((n_y,)), dma((n_y,)),
             dma((W_SLOTS, 3)),
         ],
         compiler_params=pltpu.CompilerParams(
             collective_id=2, has_side_effects=True, vmem_limit_bytes=67043328
         ),
-        name="packed_experts",
-    )(table, rows, wg, wu, wd)
+        name="packed_layer",
+    )(pos, gate, table, x_loc, wg, wu, wd)
 
 
 def solution(mesh):
@@ -782,11 +812,11 @@
         n_exp = n_loc * n_y
         capacity = CAP_FACTOR * tok // n_exp
         packed = n_loc * capacity * 5 // 8
-        rows, pos, table, most = route(x_loc, ids_loc, n_exp, capacity, packed, n_y, n_tp)
+        pos, table, most = route(ids_loc, n_exp, capacity, packed, n_y, n_tp)
 
         def by_rows():
-            y = packed_experts(table, rows, wg_loc, wu_loc, wd_loc, n_tp, capacity)
-            return combine(pos, gate_loc, y.reshape(n_y * packed, d_model))
+            gate = gate_loc.reshape(1, tok)
+            return packed_layer(pos, gate, table, x_loc, wg_loc, wu_loc, wd_loc, n_y, n_tp, packed, capacity)
 
         def by_slots():
             rows, pos = dispatch(x_loc, ids_loc, n_exp, capacity)

time: 190 us -> 166 us (0.87)
  Pallas kernels: 184 us -> 163 us
    pallas_call x2 -> x1, Pallas kernels: 167 us -> 147 us  [packed_layer(): pl.pallas_call(functools.partial(packed_kernel, n_y, n_x, packed, cap), o...]
where the time goes in v3:
time: 166 us
  Pallas kernels  163 us (98%)
  local copies, waits for them, and re-layouts  2.65 us (2%)
    pallas_call x1, Pallas kernels, packed_layer(): pl.pallas_call(functools.partial(packed_kernel, n_y, n_x, packed, cap), o...  147 us
    pallas_call x1, Pallas kernels, route(): pl.pallas_call(functools.partial(route_kernel, n_y, n_tp, n_exp, capacity...  15.9 us

profile of v3, /device:TPU:97, one launch (start us, length us, event | category | flops | bytes accessed | tf_op | source)
XLA Modules:
  0.0 166.0 jit_solution(14169395321763756842)
XLA Ops:
  0.0 15.9 %route.1 = (s32[1,1024]{1,0:T(1,128)}, s32[32,1,384]{2,1,0:T(1,128)}, s32[1,64]{1,0:T(1,128)}) custom-call(s32[1,1024]{1,0:T(1,128)} %bitcast.11), custom_call_target="tpu_custom_call" | custom-call | tf_op jit(solution)/shard_map/route/pallas_call | solution.py:422
  16.5 146.9 %conditional.1 = (bf16[1024,768]{1,0:T(8,128)(2,1)}) conditional(s32[]{:T(128)} %bitcast.6, (s32[1024,1]{0,1:T(1,128)}, bf16[1024,768]{1,0:T(8,128)(2,1)}, bf16[16,768,384]{2,1,0:T(8,128)(2,1)}, bf16[16,768,384]{2,1,0:T(8,128)(2,1)}, bf16[16,384,768]{2,1,0:T(8,128)(2,1)}, /*index=5*/f32[1024,1]{0,1:T(1,128)}) %tuple.11, (f32[1024,1]{0,1:T(1,128)}, ...), branch_computations={%region_0.0_spmd, %region_1.0_spmd} | conditional | bytes 16392 | solution.py:826
  16.7 146.7 %packed_layer.1 = bf16[1024,768]{1,0:T(8,128)(2,1)} custom-call(s32[1,1024]{1,0:T(1,128)} %get-tuple-element.42.pos_ref, f32[1,1024]{1,0:T(1,128)} %bitcast.10, s32[32,1,384]{2,1,0:T(1,128)} %get-tuple-element.44.table_ref, bf16[1024,768]{1,0:T(8,128)(2,1)} %get-tuple-element.45.x_ref, bf16[16,768,384]{2,1,0:T(8,128)(2,1)} %get-tuple-element.46.wg_hbm, ...), custom_call_target="tpu_custom_call" | custom-call | tf_op jit(solution)/shard_map/cond/branch_1_fun/packed_layer/pallas_call | solution.py:770
  163.4 2.7 %copy.15 = bf16[1024,768]{1,0:T(8,128)(2,1)} copy(bf16[1024,768]{1,0:T(8,128)(2,1)} %get-tuple-element.55) | data formatting | bytes 3145728

commit v4 on v3

--- a/solution.py
+++ b/solution.py
@@ -47,7 +47,7 @@
     )(ids_loc.reshape(1, tok), x_loc)
 
 
-def combine_kernel(pos_ref, gate_ref, y_ref, out_ref):
+def combine_kernel(pos_ref, y_ref, out_ref):
     n_slots = y_ref.shape[0]
     tok = out_ref.shape[0]
     tile = 256
@@ -57,18 +57,16 @@
         rows = pl.ds(pl.multiple_of(i * tile, tile), tile)
         pos = pos_ref[rows, :]
         pick = (lax.broadcasted_iota(jnp.int32, (tile, n_slots), 1) == pos).astype(F32).astype(BF16)
-        y = jnp.dot(pick, y_ref[...], preferred_element_type=F32)
-        weight = jnp.where(pos >= 0, gate_ref[rows, :], 0.0)
-        out_ref[rows, :] = (y * weight).astype(BF16)
-
-
-def combine(pos, gate_loc, y_slots):
-    tok = gate_loc.shape[0]
+        out_ref[rows, :] = jnp.dot(pick, y_ref[...], preferred_element_type=F32).astype(BF16)
+
+
+def combine(pos, y_slots):
+    tok = pos.shape[1]
     return pl.pallas_call(
         combine_kernel,
         out_shape=jax.ShapeDtypeStruct((tok, y_slots.shape[1]), BF16),
         name="combine",
-    )(pos.reshape(tok, 1), gate_loc, y_slots)
+    )(pos.reshape(tok, 1), y_slots)
 
 
 def expert_kernel(
@@ -323,122 +321,10 @@
     )(rows, wg, wu, wd)
 
 
-def route_kernel(
-    n_y, n_tp, n_exp, capacity, packed, ids_ref, pos_ref, table_ref, most_ref,
-    meta, col_send, col_recv, row_send, row_recv,
-):
-    tok = ids_ref.shape[1]
-    width = table_ref.shape[2]
-    n_loc = n_exp // n_y
-    yy = lax.axis_index("ep")
-    tt = lax.axis_index("tp")
-    y_peers = [(yy + d) % n_y for d in range(1, n_y)]
-    t_peers = [(tt + d) % n_tp for d in range(1, n_tp)]
-
-    barrier = pltpu.get_barrier_semaphore()
-    for device in [{"ep": p} for p in y_peers] + [{"tp": p} for p in t_peers]:
-        pl.semaphore_signal(barrier, inc=1, device_id=device, device_id_type=MESH)
-
-    ids = ids_ref[...]
-    one_hot = lax.broadcasted_iota(jnp.int32, (n_exp, tok), 0) == ids
-    before = lax.broadcasted_iota(jnp.int32, (tok, tok), 0) < lax.broadcasted_iota(jnp.int32, (tok, tok), 1)
-    before = before.astype(F32).astype(BF16)
-    preceding = jnp.dot(one_hot.astype(F32).astype(BF16), before, preferred_element_type=F32)
-    slot = jnp.sum(jnp.where(one_hot, preceding, 0.0), axis=0, keepdims=True)
-    kept = slot < capacity
-    rank = ids // n_loc
-    pad = 8
-    to_rank = (lax.broadcasted_iota(jnp.int32, (pad, tok), 0) == rank) & kept
-    ahead = jnp.dot(to_rank.astype(F32).astype(BF16), before, preferred_element_type=F32)
-    place = jnp.sum(jnp.where(to_rank, ahead, 0.0), axis=0, keepdims=True).astype(jnp.int32)
-    counts = jnp.sum(to_rank.astype(F32), axis=1, keepdims=True)
-    most = jnp.max(counts, axis=0, keepdims=True).astype(jnp.int32)
-    fits = kept & (place < packed)
-    pos = jnp.where(fits, rank * packed + place, -1)
-    pos_ref[...] = pos
-    row_id = lax.broadcasted_iota(jnp.int32, (pad, tok), 0)
-    parts = jnp.where(row_id == 0, (ids % n_loc).astype(F32), jnp.where(row_id == 1, slot, 1.0))
-    parts = jnp.where(kept, parts, 0.0).astype(BF16)
-
-    @pl.loop(0, n_y)
-    def _(r):
-        pick = (lax.broadcasted_iota(jnp.int32, (packed, tok), 0) + r * packed) == pos
-        pick = pick.astype(F32).astype(BF16)
-        got = lax.dot_general(parts, pick, (((1,), (1,)), ((), ())), preferred_element_type=F32)
-        where = jnp.where(got[2:3] > 0.5, got[0:1] * capacity + got[1:2], -1.0)
-        meta[r, :, 0:packed] = where.astype(jnp.int32)
-        meta[r, :, packed:width] = jnp.broadcast_to(most, (1, width - packed))
-
-    pl.semaphore_wait(barrier, len(y_peers) + len(t_peers))
-    table_ref[pl.ds(tt * n_y + yy, 1)] = meta[pl.ds(yy, 1)]
-
-    def col_copy(k):
-        return pltpu.make_async_remote_copy(
-            src_ref=meta.at[y_peers[k]], dst_ref=table_ref.at[tt * n_y + yy],
-            send_sem=col_send.at[k], recv_sem=col_recv.at[k], device_id={"ep": y_peers[k]}, device_id_type=MESH,
-        )
-
-    def col_arrival(k):
-        src = (yy + n_y - 1 - k) % n_y
-        return pltpu.make_async_remote_copy(
-            src_ref=meta.at[src], dst_ref=table_ref.at[tt * n_y + src],
-            send_sem=col_send.at[k], recv_sem=col_recv.at[k], device_id={"ep": src}, device_id_type=MESH,
-        )
-
-    def row_copy(k):
-        view = table_ref.at[pl.ds(tt * n_y, n_y)]
-        return pltpu.make_async_remote_copy(
-            src_ref=view, dst_ref=view,
-            send_sem=row_send.at[k], recv_sem=row_recv.at[k], device_id={"tp": t_peers[k]}, device_id_type=MESH,
-        )
-
-    def row_arrival(k):
-        src = (tt + n_tp - 1 - k) % n_tp
-        view = table_ref.at[pl.ds(src * n_y, n_y)]
-        return pltpu.make_async_remote_copy(
-            src_ref=view, dst_ref=view,
-            send_sem=row_send.at[k], recv_sem=row_recv.at[k], device_id={"tp": src}, device_id_type=MESH,
-        )
-
-    for k in range(len(y_peers)):
-        col_copy(k).start()
-    for k in range(len(y_peers)):
-        col_arrival(k).wait_recv()
-    for k in range(len(t_peers)):
-        row_copy(k).start()
-    for k in range(len(t_peers)):
-        row_arrival(k).wait_recv()
-    most_ref[...] = jnp.max(table_ref[:, :, packed:width], axis=0)
-    for k in range(len(y_peers)):
-        col_copy(k).wait_send()
-    for k in range(len(t_peers)):
-        row_copy(k).wait_send()
-
-
-def route(ids_loc, n_exp, capacity, packed, n_y, n_tp):
-    tok = ids_loc.shape[0]
-    width = -(-(packed + 1) // 128) * 128
-    dma = pltpu.SemaphoreType.DMA
-    return pl.pallas_call(
-        functools.partial(route_kernel, n_y, n_tp, n_exp, capacity, packed),
-        out_shape=(
-            jax.ShapeDtypeStruct((1, tok), jnp.int32),
-            jax.ShapeDtypeStruct((n_y * n_tp, 1, width), jnp.int32),
-            jax.ShapeDtypeStruct((1, width - packed), jnp.int32),
-        ),
-        scratch_shapes=[
-            pltpu.VMEM((n_y, 1, width), jnp.int32),
-            dma((n_y - 1,)), dma((n_y - 1,)), dma((n_tp - 1,)), dma((n_tp - 1,)),
-        ],
-        compiler_params=pltpu.CompilerParams(collective_id=1, has_side_effects=True),
-        name="route",
-    )(ids_loc.reshape(1, tok))
-
-
 def packed_kernel(
-    n_y, n_x, packed, cap, pos_ref, gate_ref, table_ref, x_ref, wg_hbm, wu_hbm, wd_hbm, out_ref,
-    pack_buf, x_buf, slot_buf, pair_buf, opp_buf, nbr_buf, ret_buf, w_in, w_out, pos_col, gate_col,
-    ys_send, ys_recv, a_send, a_recv, b_send, b_recv, s_send, s_recv,
+    n_y, n_x, packed, cap, ids_ref, x_ref, wg_hbm, wu_hbm, wd_hbm, out_ref, most_ref,
+    pack_buf, x_buf, slot_buf, pair_buf, opp_buf, nbr_buf, ret_buf, w_in, w_out, pos_col,
+    lists, table, flags, l_send, l_recv, t_send, t_recv, m_send, m_recv, ys_send, ys_recv, a_send, a_recv, b_send, b_recv, s_send, s_recv,
     p_send, p_recv, e_send, e_recv, n_send, n_recv, f_send, f_recv, h_send, h_recv, w_sem,
 ):
     tok, d_model = x_ref.shape
@@ -454,9 +340,12 @@
     xx, cc = tt // 2, tt % 2
     xr, xl, xo = (xx + 1) % n_x, (xx + n_x - 1) % n_x, (xx + 2) % n_x
     right, left, mate = {"tp": xr * 2 + cc}, {"tp": xl * 2 + cc}, {"tp": xx * 2 + 1 - cc}
+    across = {"tp": xo * 2 + cc}
     sides = (right, left)
     ahead, behind = (xr, xl), (xl, xr)
     mine, other = cc * n_x, (1 - cc) * n_x
+    width = table.shape[3]
+    n_exp = n_loc * n_y
 
     def row_of(t):
         return (yy + t + cc * (n_y - 2 * t) + n_y) % n_y
@@ -474,6 +363,20 @@
 
     def y_copy(t):
         return remote(pack_buf.at[t], x_buf.at[t, xx], ys_send.at[t], ys_recv.at[t], {"ep": row_to(t)})
+
+    def list_copy(t):
+        return remote(lists.at[t], table.at[t, xx], l_send.at[t], l_recv.at[t], {"ep": row_to(t)})
+
+    def table_copy(t, k):
+        view = table.at[t, xx]
+        return remote(view, view, t_send.at[t, k], t_recv.at[t, k], (right, left, across)[k])
+
+    def table_arrival(t, k):
+        view = table.at[t, (xl, xr, xo)[k]]
+        return remote(view, view, t_send.at[t, k], t_recv.at[t, k], (right, left, across)[k])
+
+    def flag_copy():
+        return remote(flags.at[0], flags.at[1], m_send, m_recv, mate)
 
     def a_copy(t, k, h):
         view = x_buf.at[t, xx, part(h)]
@@ -532,18 +435,56 @@
         )
 
     barrier = pltpu.get_barrier_semaphore()
-    for device in [right, left, mate] + [{"ep": (yy + d) % n_y} for d in range(1, n_y)]:
+    for device in [right, left, across, mate] + [{"ep": (yy + d) % n_y} for d in range(1, n_y)]:
         pl.semaphore_signal(barrier, inc=1, device_id=device, device_id_type=MESH)
+    for w in range(W_SLOTS):
+        for c in w_copies(w):
+            c.start()
+
+    ids = ids_ref[...]
+    one_hot = lax.broadcasted_iota(jnp.int32, (n_exp, tok), 0) == ids
+    earlier = lax.broadcasted_iota(jnp.int32, (tok, tok), 0) < lax.broadcasted_iota(jnp.int32, (tok, tok), 1)
+    earlier = earlier.astype(F32).astype(BF16)
+    preceding = jnp.dot(one_hot.astype(F32).astype(BF16), earlier, preferred_element_type=F32)
+    slot = jnp.sum(jnp.where(one_hot, preceding, 0.0), axis=0, keepdims=True)
+    kept = slot < cap
+    rank = ids // n_loc
+    pad = 8
+    to_rank = (lax.broadcasted_iota(jnp.int32, (pad, tok), 0) == rank) & kept
+    before = jnp.dot(to_rank.astype(F32).astype(BF16), earlier, preferred_element_type=F32)
+    place = jnp.sum(jnp.where(to_rank, before, 0.0), axis=0, keepdims=True).astype(jnp.int32)
+    counts = jnp.sum(to_rank.astype(F32), axis=1, keepdims=True)
+    most = jnp.max(counts, axis=0, keepdims=True).astype(jnp.int32)
+    pos = jnp.where(kept & (place < packed), rank * packed + place, -1)
+    row_id = lax.broadcasted_iota(jnp.int32, (pad, tok), 0)
+    parts = jnp.where(row_id == 0, (ids % n_loc).astype(F32), jnp.where(row_id == 1, slot, 1.0))
+    parts = jnp.where(kept, parts, 0.0).astype(BF16)
+
+    def wanted(t):
+        pick = (lax.broadcasted_iota(jnp.int32, (packed, tok), 0) + row_to(t) * packed) == pos
+        return pick.astype(F32).astype(BF16)
 
     def pack(t):
-        first = row_to(t) * packed
-        pick = (lax.broadcasted_iota(jnp.int32, (packed, tok), 0) + first) == pos_ref[...]
-        return jnp.dot(pick.astype(F32).astype(BF16), x_ref[...], preferred_element_type=F32).astype(BF16)
+        return jnp.dot(wanted(t), x_ref[...], preferred_element_type=F32).astype(BF16)
+
+    def list_of(t):
+        got = lax.dot_general(parts, wanted(t), (((1,), (1,)), ((), ())), preferred_element_type=F32)
+        return jnp.where(got[2:3] > 0.5, got[0:1] * cap + got[1:2], -1.0).astype(jnp.int32)
+
+    def send_half(t, h):
+        for k in range(2):
+            a_copy(t, k, h if k == 0 else 1 - h).start()
+
+    def send_table(t):
+        for k in (2, 0, 1):
+            table_copy(t, k).start()
 
     def send_own(t):
-        for h in range(2):
-            for k in range(2):
-                a_copy(t, k, h if k == 0 else 1 - h).start()
+        list_copy(t).wait_recv()
+        send_table(t)
+        y_copy(t).wait_recv()
+        send_half(t, 0)
+        send_half(t, 1)
 
     def pass_on(t):
         for k in range(2):
@@ -551,8 +492,7 @@
             b_copy(t, k).start()
 
     def source_row(t, b):
-        row = table_ref[(b * 2 + cc) * n_y + row_of(t)]
-        return row[:, :packed]
+        return table[t, b][:, :packed]
 
     def spread(t, blocks):
         @pl.loop(0, len(blocks))
@@ -568,6 +508,7 @@
 
     def share(t):
         for k in range(2):
+            table_arrival(t, k).wait_recv()
             a_arrival(t, k, 1 - k).wait_recv()
         spread(t, (xl, xr))
 
@@ -618,6 +559,8 @@
         for k in range(2):
             e_copy(t, k).start()
         gather_back(t, (xr, xl))
+
+    def early_sums(t):
         for k in range(2):
             n_copy(t, k).start()
 
@@ -639,9 +582,7 @@
             x_buf[t, xx] = total.astype(BF16)
             h_copy(t).start()
 
-    def combine_into(t, first, last):
-        if not isinstance(t, int) or t > 0:
-            h_copy(t).wait_recv()
+    def combine_into(t, first):
         tile = 256
 
         @pl.loop(0, tok // tile)
@@ -655,39 +596,36 @@
             y = jnp.dot(pick[:, :packed].astype(BF16), ret_buf[t], preferred_element_type=F32)
             if not first:
                 y = y + out_ref[rows, :].astype(F32)
-            if last:
-                weight = jnp.where(pos_col[rows, 0:1] >= 0, gate_col[rows, 0:1], 0.0)
-                y = y * weight
             out_ref[rows, :] = y.astype(BF16)
 
     x_buf[0, xx] = pack(0)
-    pl.semaphore_wait(barrier, 2 + n_y)
-    send_own(0)
+    pl.semaphore_wait(barrier, 3 + n_y)
+    send_half(0, 0)
+    table[0, xx, :, 0:packed] = list_of(0)
+    table[0, xx, :, packed:width] = jnp.broadcast_to(most, (1, width - packed))
+    send_table(0)
+    send_half(0, 1)
 
     @pl.loop(1, n_y)
     def _(t):
+        lists[t, :, 0:packed] = list_of(t)
+        lists[t, :, packed:width] = jnp.broadcast_to(most, (1, width - packed))
+        list_copy(t).start()
         pack_buf[t] = pack(t)
         y_copy(t).start()
 
-    for w in range(W_SLOTS):
-        for c in w_copies(w):
-            c.start()
     spread(0, (xx,))
     pass_on(0)
-    y_copy(1).wait_recv()
     send_own(1)
     tile = 256
-
-    @pl.loop(0, tok // tile)
-    def _(i):
-        rows = pl.ds(pl.multiple_of(i * tile, tile), tile)
-        pos_col[rows, :] = jnp.transpose(jnp.broadcast_to(pos_ref[:, rows].astype(F32), (128, tile)))
-        gate_col[rows, :] = jnp.transpose(jnp.broadcast_to(gate_ref[:, rows], (128, tile)))
-
+    for i in range(tok // tile):
+        spot = pos[:, i * tile:(i + 1) * tile].astype(F32)
+        pos_col[i * tile:(i + 1) * tile, :] = jnp.transpose(jnp.broadcast_to(spot, (128, tile)))
     share(0)
 
     @pl.loop(0, n_y)
     def _(t):
+        table_arrival(t, 2).wait_recv()
         for k in range(2):
             b_arrival(t, k).wait_recv()
         spread(t, (xo,))
@@ -698,7 +636,6 @@
 
         @pl.when(t + 2 < n_y)
         def _():
-            y_copy(t + 2).wait_recv()
             send_own(t + 2)
 
         for b in range(n_x):
@@ -712,7 +649,7 @@
 
         multiply(t, n_grp // 2, n_grp)
 
-        @pl.when(t > 0)
+        @pl.when(t > 1)
         def _():
             last_sums(t - 1)
 
@@ -725,53 +662,68 @@
                 a_copy(t, k, h).wait_send()
             b_copy(t, k).wait_send()
         first_sums(t)
+
+        @pl.when(t > 0)
+        def _():
+            early_sums(t)
+
         gather_back(t, (xx,))
 
         @pl.loop(0, n_grp)
         def _(i):
             p_copy(t, i).wait_send()
 
-        @pl.when(t == 2)
-        def _():
-            give_back(0, True)
-
         @pl.when(t > 2)
         def _():
             give_back(t - 2, False)
 
+    top = jnp.max(table[:, :, 0, packed:width])
+    flags[0] = jnp.full((1, 128), top, jnp.int32)
+    flag_copy().start()
     last_sums(n_y - 1)
-    for t in range(max(n_y - 2, 0), n_y):
-        if t == n_y - 1:
-            combine_into(0, True, False)
-        give_back(t, t == 0)
+    early_sums(0)
+    last_sums(0)
+    for t in range(1, n_y + 1):
+        if n_y - 2 <= t < n_y:
+            give_back(t, False)
+        if t > 1:
+            h_copy(t - 1).wait_recv()
+            combine_into(t - 1, t == 2)
+    flag_copy().wait()
+    most_ref[...] = jnp.maximum(flags[0], flags[1])
     for t in range(1, n_y):
-        combine_into(t, False, t == n_y - 1)
-    for t in range(1, n_y):
+        list_copy(t).wait_send()
         y_copy(t).wait_send()
         h_copy(t).wait_send()
 
     @pl.loop(0, n_y)
     def _(t):
+        for k in range(3):
+            table_copy(t, k).wait_send()
         for k in range(2):
             e_copy(t, k).wait_send()
             n_copy(t, k).wait_send()
             f_copy(t, k).wait_send()
 
-
-def packed_layer(pos, gate, table, x_loc, wg, wu, wd, n_y, n_tp, packed, cap):
+    give_back(0, True)
+    combine_into(0, False)
+
+
+def packed_layer(ids_loc, x_loc, wg, wu, wd, n_y, n_tp, packed, cap):
     tok, d_model = x_loc.shape
     n_loc, _, hidden = wg.shape
     n_x = n_tp // 2
     n_grp = n_loc // GROUP
     half = packed // 2
+    width = -(-(packed + 1) // 128) * 128
     dma = pltpu.SemaphoreType.DMA
     hbm = pl.BlockSpec(memory_space=pltpu.HBM)
     vmem = pl.BlockSpec(memory_space=pltpu.VMEM)
     return pl.pallas_call(
         functools.partial(packed_kernel, n_y, n_x, packed, cap),
-        out_shape=jax.ShapeDtypeStruct((tok, d_model), BF16),
-        in_specs=[vmem] * 4 + [hbm] * 3,
-        out_specs=vmem,
+        out_shape=(jax.ShapeDtypeStruct((tok, d_model), BF16), jax.ShapeDtypeStruct((1, 128), jnp.int32)),
+        in_specs=[vmem] * 2 + [hbm] * 3,
+        out_specs=(vmem, vmem),
         scratch_shapes=[
             pltpu.VMEM((n_y, packed, d_model), BF16),
             pltpu.VMEM((n_y, n_x, packed, d_model), BF16),
@@ -783,7 +735,10 @@
             pltpu.VMEM((W_SLOTS, GROUP, d_model, 2 * hidden), BF16),
             pltpu.VMEM((W_SLOTS, GROUP, hidden, d_model), BF16),
             pltpu.VMEM((tok, 128), F32),
-            pltpu.VMEM((tok, 128), F32),
+            pltpu.VMEM((n_y, 1, width), jnp.int32),
+            pltpu.VMEM((n_y, n_x, 1, width), jnp.int32),
+            pltpu.VMEM((2, 1, 128), jnp.int32),
+            dma((n_y,)), dma((n_y,)), dma((n_y, 3)), dma((n_y, 3)), dma, dma,
             dma((n_y,)), dma((n_y,)),
             dma((n_y, 2, 2)), dma((n_y, 2, 2)),
             dma((n_y, 2)), dma((n_y, 2)),
@@ -799,7 +754,7 @@
             collective_id=2, has_side_effects=True, vmem_limit_bytes=67043328
         ),
         name="packed_layer",
-    )(pos, gate, table, x_loc, wg, wu, wd)
+    )(ids_loc.reshape(1, tok), x_loc, wg, wu, wd)
 
 
 def solution(mesh):
@@ -812,17 +767,14 @@
         n_exp = n_loc * n_y
         capacity = CAP_FACTOR * tok // n_exp
         packed = n_loc * capacity * 5 // 8
-        pos, table, most = route(ids_loc, n_exp, capacity, packed, n_y, n_tp)
-
-        def by_rows():
-            gate = gate_loc.reshape(1, tok)
-            return packed_layer(pos, gate, table, x_loc, wg_loc, wu_loc, wd_loc, n_y, n_tp, packed, capacity)
-
-        def by_slots():
+        picked, most = packed_layer(ids_loc, x_loc, wg_loc, wu_loc, wd_loc, n_y, n_tp, packed, capacity)
+
+        def by_slots(carry):
             rows, pos = dispatch(x_loc, ids_loc, n_exp, capacity)
             y = experts(rows.reshape(n_exp, capacity, d_model), wg_loc, wu_loc, wd_loc, n_y, n_tp)
-            return combine(pos, gate_loc, y.reshape(n_exp * capacity, d_model))
-
-        return lax.cond(most[0, 0] <= packed, by_rows, by_slots)
+            return combine(pos, y.reshape(n_exp * capacity, d_model)), jnp.int32(0)
+
+        picked, _ = lax.while_loop(lambda carry: carry[1] > packed, by_slots, (picked, most[0, 0]))
+        return (picked.astype(F32) * gate_loc).astype(BF16)
 
     return jax.shard_map(local_layer, mesh=mesh, in_specs=(row_spec, row_spec, row_spec, P("ep", None, "tp"), P("ep", None, "tp"), P("ep", "tp", None)), out_specs=row_spec, check_vma=False)

time: 166 us -> 148 us (0.89)
  Pallas kernels: 163 us -> 144 us
  other arithmetic: 0 us -> 2.88 us
  local copies, waits for them, and re-layouts: 2.65 us -> 0 us
    pallas_call x1 -> x0, Pallas kernels: 15.9 us -> none  [route(): pl.pallas_call(functools.partial(route_kernel, n_y, n_tp, n_exp, capacity...]
    convert_element_type x0 -> x1, other arithmetic: none -> 2.88 us  [local_layer(): return (picked.astype(F32) * gate_loc).astype(BF16)]
    pallas_call x1, Pallas kernels: 147 us -> 144 us  [packed_layer(): pl.pallas_call(functools.partial(packed_kernel, n_y, n_x, packed, cap), o...]
    unnamed x1 -> x0, local copies, waits for them, and re-layouts: 2.65 us -> none
where the time goes in v4:
time: 148 us
  Pallas kernels  144 us (97%)
  other arithmetic  2.88 us (2%)
    pallas_call x1, Pallas kernels, packed_layer(): pl.pallas_call(functools.partial(packed_kernel, n_y, n_x, packed, cap), o...  144 us

profile of v4, /device:TPU:97, one launch (start us, length us, event | category | flops | bytes accessed | tf_op | source)
XLA Modules:
  0.0 147.5 jit_solution(964531736674302418)
XLA Ops:
  0.0 143.8 %packed_layer.1 = (bf16[1024,768]{1,0:T(8,128)(2,1)}, s32[1,128]{1,0:T(1,128)}) custom-call(s32[1,1024]{1,0:T(1,128)} %bitcast.10, bf16[1024,768]{1,0:T(8,128)(2,1)} %x_ref.1, bf16[16,768,384]{2,1,0:T(8,128)(2,1)} %wg_hbm.1, bf16[16,768,384]{2,1,0:T(8,128)(2,1)} %wu_hbm.1, bf16[16,384,768]{2,1,0:T(8,128)(2,1)} %wd_hbm.1), custom_call_target="tpu_custom_call" | custom-call | tf_op jit(solution)/shard_map/packed_layer/pallas_call | solution.py:722
  143.8 0.8 while.9
  144.6 2.9 %multiply_convert_fusion = bf16[1024,768]{1,0:T(8,128)(2,1)} fusion(bf16[1024,768]{1,0:T(8,128)(2,1)} %get-tuple-element.46, f32[1024]{0:T(1024)} %bitcast.13), kind=kLoop, calls=%fused_computation | loop fusion | flops 2359296 | bytes 3149824 | tf_op jit(solution)/shard_map/convert_element_type | solution.py:778

commit v5 on v4

v5 whole, which is shorter than its diff:
```python
import functools

import jax
import jax.numpy as jnp
from jax import lax
from jax.experimental import pallas as pl
from jax.experimental.pallas import tpu as pltpu
from jax.sharding import PartitionSpec as P

CAP_FACTOR = 2
GROUP = 2
W_SLOTS = 4
EXTRA = 64
VMEM_LIMIT = 59 * 2**20
MESH = pl.DeviceIdType.MESH
BF16 = jnp.bfloat16
F32 = jnp.float32


def halves(packed):
    first = -(-packed // 32) * 16
    return first, packed - first


def packed_kernel(
    n_y, n_x, packed, cap, base_ref, ids_ref, gate_ref, x_ref, wg_hbm, wu_hbm, wd_hbm, out_ref, most_ref,
    pack_buf, x_buf, slot_buf, pair_buf, opp_buf, nbr_buf, ret_buf, w_in, w_out, pos_col, gate_col,
    lists, table, flags, l_send, l_recv, t_send, t_recv, m_send, m_recv, ys_send, ys_recv, a_send, a_recv, b_send, b_recv, s_send, s_recv,
    p_send, p_recv, e_send, e_recv, n_send, n_recv, f_send, f_recv, h_send, h_recv, w_sem,
):
    tok, d_model = x_ref.shape
    n_loc = slot_buf.shape[1]
    n_slots = n_loc * cap
    hidden = w_out.shape[2]
    sizes = halves(packed)
    n_src = 2 * n_x
    n_grp = n_loc // GROUP
    n_w = n_y * n_grp
    yy = lax.axis_index("ep")
    tt = lax.axis_index("tp")
    xx, cc = tt // 2, tt % 2
    xr, xl, xo = (xx + n_x + 1 - 2 * cc) % n_x, (xx + n_x - 1 + 2 * cc) % n_x, (xx + 2) % n_x
    right, left, mate = {"tp": xr * 2 + cc}, {"tp": xl * 2 + cc}, {"tp": xx * 2 + 1 - cc}
    across = {"tp": xo * 2 + cc}
    sides = (right, left)
    ahead, behind = (xr, xl), (xl, xr)
    mine, other = cc * n_x, (1 - cc) * n_x
    width = table.shape[3]
    n_exp = n_loc * n_y

    def row_of(t):
        return (yy + t + cc * (n_y - 2 * t) + n_y) % n_y

    def row_to(t):
        return (yy - t - cc * (n_y - 2 * t) + 2 * n_y) % n_y

    def remote(src, dst, send, recv, device):
        return pltpu.make_async_remote_copy(
            src_ref=src, dst_ref=dst, send_sem=send, recv_sem=recv, device_id=device, device_id_type=MESH
        )

    def part(h):
        return pl.ds(h * sizes[0], sizes[h])

    def y_copy(t):
        return remote(pack_buf.at[t], x_buf.at[t, xx], ys_send.at[t], ys_recv.at[t], {"ep": row_to(t)})

    def list_copy(t):
        return remote(lists.at[t], table.at[t, xx], l_send.at[t], l_recv.at[t], {"ep": row_to(t)})

    def table_copy(t, k):
        view = table.at[t, xx]
        return remote(view, view, t_send.at[t, k], t_recv.at[t, k], (right, left, across)[k])

    def table_arrival(t, k):
        view = table.at[t, (xl, xr, xo)[k]]
        return remote(view, view, t_send.at[t, k], t_recv.at[t, k], (right, left, across)[k])

    def flag_copy():
        return remote(flags.at[0], flags.at[1], m_send, m_recv, mate)

    def a_copy(t, k, h):
        view = x_buf.at[t, xx, part(h)]
        return remote(view, view, a_send.at[t, k, h], a_recv.at[t, k, h], sides[k])

    def a_arrival(t, k, h):
        view = x_buf.at[t, behind[k], part(h)]
        return remote(view, view, a_send.at[t, k, h], a_recv.at[t, k, h], sides[k])

    def b_copy(t, k):
        view = x_buf.at[t, behind[k], part(k)]
        return remote(view, view, b_send.at[t, k], b_recv.at[t, k], sides[k])

    def b_arrival(t, k):
        view = x_buf.at[t, xo, part(k)]
        return remote(view, view, b_send.at[t, k], b_recv.at[t, k], sides[k])

    def s_copy(t, b):
        view = slot_buf.at[t % 2, :, mine + b]
        return remote(view, view, s_send.at[t, b], s_recv.at[t, b], mate)

    def s_arrival(t, b):
        view = slot_buf.at[t % 2, :, other + b]
        return remote(view, view, s_send.at[t, b], s_recv.at[t, b], mate)

    def p_copy(t, i):
        at = pl.ds(i * GROUP, GROUP)
        return remote(
            slot_buf.at[t % 2, at, pl.ds(other, n_x)], pair_buf.at[t % 2, at], p_send.at[t, i], p_recv.at[t, i], mate
        )

    def e_copy(t, k):
        dst = opp_buf.at[k, t, pl.ds(0, sizes[k])]
        return remote(x_buf.at[t, xo, part(k)], dst, e_send.at[t, k], e_recv.at[t, k], sides[k])

    def n_copy(t, k):
        h = 1 - k
        return remote(
            x_buf.at[t, ahead[k], part(h)], nbr_buf.at[k, t, part(h)], n_send.at[t, k], n_recv.at[t, k], sides[k]
        )

    def f_copy(t, k):
        return remote(
            x_buf.at[t, ahead[k], part(k)], nbr_buf.at[k, t, part(k)], f_send.at[t, k], f_recv.at[t, k], sides[k]
        )

    def h_copy(t):
        return remote(x_buf.at[t, xx], ret_buf.at[t], h_send.at[t], h_recv.at[t], {"ep": row_of(t)})

    def w_copies(w):
        s = w % W_SLOTS
        at = pl.ds((w % n_grp) * GROUP, GROUP)
        return (
            pltpu.make_async_copy(wg_hbm.at[at], w_in.at[s, :, :, pl.ds(0, hidden)], w_sem.at[s, 0]),
            pltpu.make_async_copy(wu_hbm.at[at], w_in.at[s, :, :, pl.ds(hidden, hidden)], w_sem.at[s, 1]),
            pltpu.make_async_copy(wd_hbm.at[at], w_out.at[s], w_sem.at[s, 2]),
        )

    barrier = pltpu.get_barrier_semaphore()
    for device in [right, left, across, mate] + [{"ep": (yy + d) % n_y} for d in range(1, n_y)]:
        pl.semaphore_signal(barrier, inc=1, device_id=device, device_id_type=MESH)
    for w in range(W_SLOTS):
        for c in w_copies(w):
            c.start()

    ids = ids_ref[...]
    lanes = 128
    order = (lax.broadcasted_iota(jnp.int32, (lanes, 2 * lanes), 0), lax.broadcasted_iota(jnp.int32, (lanes, 2 * lanes), 1))
    earlier = ((order[0] < order[1]) | (order[1] >= lanes)).astype(F32).astype(BF16)

    def count_left(marks):
        n = marks.shape[0]
        tiles = [marks[:, i * lanes:(i + 1) * lanes] for i in range(tok // lanes)]
        both = jnp.dot(jnp.concatenate(tiles, axis=0).astype(BF16), earlier, preferred_element_type=F32)
        total, left = jnp.zeros((n, lanes), F32), []
        for i in range(len(tiles)):
            left.append(both[i * n:(i + 1) * n, :lanes] + total)
            total = total + both[i * n:(i + 1) * n, lanes:]
        return jnp.concatenate(left, axis=1), total

    one_hot = lax.broadcasted_iota(jnp.int32, (n_exp, tok), 0) == ids
    preceding, _ = count_left(one_hot.astype(F32))
    slot = jnp.sum(jnp.where(one_hot, preceding, 0.0), axis=0, keepdims=True)
    kept = slot < cap
    rank = ids // n_loc
    pad = 8
    to_rank = (lax.broadcasted_iota(jnp.int32, (pad, tok), 0) == rank) & kept
    before, counts = count_left(to_rank.astype(F32))
    place = jnp.sum(jnp.where(to_rank, before, 0.0), axis=0, keepdims=True).astype(jnp.int32) - base_ref[0]
    most = jnp.max(counts, axis=0, keepdims=True).astype(jnp.int32)[:, 0:width - packed]
    pos = jnp.where(kept & (place >= 0) & (place < packed), rank * packed + place, -1)
    row_id = lax.broadcasted_iota(jnp.int32, (pad, tok), 0)
    parts = jnp.where(row_id == 0, (ids % n_loc).astype(F32), jnp.where(row_id == 1, slot, 1.0))
    parts = jnp.where(kept, parts, 0.0).astype(BF16)

    def wanted(t):
        pick = (lax.broadcasted_iota(jnp.int32, (packed, tok), 0) + row_to(t) * packed) == pos
        return pick.astype(F32).astype(BF16)

    def pack(t):
        return jnp.dot(wanted(t), x_ref[...], preferred_element_type=F32).astype(BF16)

    def list_of(t):
        got = lax.dot_general(parts, wanted(t), (((1,), (1,)), ((), ())), preferred_element_type=F32)
        return jnp.where(got[2:3] > 0.5, got[0:1] * cap + got[1:2], -1.0).astype(jnp.int32)

    def send_half(t, h):
        for k in range(2):
            a_copy(t, k, h if k == 0 else 1 - h).start()

    def send_table(t):
        for k in (2, 0, 1):
            table_copy(t, k).start()

    def send_own(t):
        list_copy(t).wait_recv()
        send_table(t)
        y_copy(t).wait_recv()
        send_half(t, 0)
        send_half(t, 1)

    def pass_on(t):
        for k in range(2):
            a_arrival(t, k, k).wait_recv()
            b_copy(t, k).start()

    def source_row(t, b):
        return table[t, b][:, :packed]

    def spread(t, blocks):
        @pl.loop(0, len(blocks))
        def _(j):
            b = blocks[0]
            for n, blk in enumerate(blocks[1:]):
                b = jnp.where(j == n + 1, blk, b)
            to = source_row(t, b)
            pick = (lax.broadcasted_iota(jnp.int32, (n_slots, packed), 0) == to).astype(F32).astype(BF16)
            slots = jnp.dot(pick, x_buf[t, b], preferred_element_type=F32).astype(BF16)
            slot_buf[t % 2, :, mine + b] = slots.reshape(n_loc, cap, d_model)
            s_copy(t, b).start()

    def share(t):
        for k in range(2):
            table_arrival(t, k).wait_recv()
            a_arrival(t, k, 1 - k).wait_recv()
        spread(t, (xl, xr))

    def multiply(t, lo, hi):
        @pl.loop(lo, hi)
        def _(i):
            w = t * n_grp + i
            s = w % W_SLOTS
            for c in w_copies(w):
                c.wait()
            both = []
            for el in range(GROUP):
                tile = slot_buf[t % 2, i * GROUP + el].reshape(n_src * cap, d_model)
                both.append(jnp.dot(tile, w_in[s, el], preferred_element_type=F32))
            for el in range(GROUP):
                act = (jax.nn.silu(both[el][:, :hidden]) * both[el][:, hidden:]).astype(BF16)
                out = jnp.dot(act, w_out[s, el], preferred_element_type=F32)
                slot_buf[t % 2, i * GROUP + el] = out.astype(BF16).reshape(n_src, cap, d_model)
            p_copy(t, i).start()

            @pl.when(w + W_SLOTS < n_w)
            def _():
                for c in w_copies(w + W_SLOTS):
                    c.start()

    def gather_back(t, blocks):
        @pl.loop(0, len(blocks))
        def _(j):
            b = blocks[0]
            for n, blk in enumerate(blocks[1:]):
                b = jnp.where(j == n + 1, blk, b)
            to = source_row(t, b).astype(F32)
            col = jnp.transpose(jnp.broadcast_to(to, (128, packed)))
            lane = lax.broadcasted_iota(jnp.int32, (packed, 128), 1).astype(F32)
            pick = jnp.concatenate(
                [(col == lane + float(128 * m)).astype(F32).astype(BF16) for m in range(n_slots // 128)], axis=1
            )
            total = slot_buf[t % 2, :, mine + b].astype(F32) + pair_buf[t % 2, :, b].astype(F32)
            slots = total.astype(BF16).reshape(n_slots, d_model)
            x_buf[t, b] = jnp.dot(pick, slots, preferred_element_type=F32).astype(BF16)

    def first_sums(t):
        @pl.loop(0, n_grp)
        def _(i):
            p_copy(t, i).wait_recv()

        gather_back(t, (xo,))
        for k in range(2):
            e_copy(t, k).start()
        gather_back(t, (xr, xl))

    def early_sums(t):
        for k in range(2):
            n_copy(t, k).start()

    def last_sums(t):
        for k in range(2):
            e_copy(t, k).wait_recv()
            at = (t, ahead[k], part(k))
            x_buf[at] = (x_buf[at].astype(F32) + opp_buf[k, t, pl.ds(0, sizes[k])].astype(F32)).astype(BF16)
            f_copy(t, k).start()

    def give_back(t, local):
        for k in range(2):
            n_copy(t, k).wait_recv()
            f_copy(t, k).wait_recv()
        total = x_buf[t, xx].astype(F32) + (nbr_buf[0, t].astype(F32) + nbr_buf[1, t].astype(F32))
        if local:
            ret_buf[t] = total.astype(BF16)
        else:
            x_buf[t, xx] = total.astype(BF16)
            h_copy(t).start()

    def combine_into(t, first):
        tile = 256

        @pl.loop(0, tok // tile)
        def _(i):
            rows = pl.ds(pl.multiple_of(i * tile, tile), tile)
            want = pos_col[rows, :] - (row_to(t) * packed).astype(F32)
            lane = lax.broadcasted_iota(jnp.int32, (tile, 128), 1).astype(F32)
            pick = jnp.concatenate(
                [(want == lane + float(128 * m)).astype(F32) for m in range(-(-packed // 128))], axis=1
            )
            y = jnp.dot(pick[:, :packed].astype(BF16), ret_buf[t], preferred_element_type=F32)
            gate = gate_col[rows, :]
            y = jnp.concatenate([y[:, m * 128:(m + 1) * 128] * gate for m in range(d_model // 128)], axis=1)
            if not first:
                y = y + out_ref[rows, :].astype(F32)
            out_ref[rows, :] = y.astype(BF16)

    x_buf[0, xx] = pack(0)
    pl.semaphore_wait(barrier, 3 + n_y)
    send_half(0, 0)
    table[0, xx, :, 0:packed] = list_of(0)
    table[0, xx, :, packed:width] = most
    send_table(0)
    send_half(0, 1)

    @pl.loop(1, n_y)
    def _(t):
        lists[t, :, 0:packed] = list_of(t)
        lists[t, :, packed:width] = most
        list_copy(t).start()
        pack_buf[t] = pack(t)
        y_copy(t).start()

    spread(0, (xx,))
    pass_on(0)
    send_own(1)
    tile = 256
    for i in range(tok // tile):
        spot = pos[:, i * tile:(i + 1) * tile].astype(F32)
        pos_col[i * tile:(i + 1) * tile, :] = jnp.transpose(jnp.broadcast_to(spot, (128, tile)))
        gate = gate_ref[:, i * tile:(i + 1) * tile]
        gate_col[i * tile:(i + 1) * tile, :] = jnp.transpose(jnp.broadcast_to(gate, (128, tile)))
    share(0)

    @pl.loop(0, n_y)
    def _(t):
        table_arrival(t, 2).wait_recv()
        for k in range(2):
            b_arrival(t, k).wait_recv()
        spread(t, (xo,))

        @pl.when(t + 1 < n_y)
        def _():
            pass_on(t + 1)

        @pl.when(t + 2 < n_y)
        def _():
            send_own(t + 2)

        for b in range(n_x):
            s_arrival(t, b).wait_recv()
            s_copy(t, b).wait_send()
        multiply(t, 0, n_grp // 2)

        @pl.when(t + 1 < n_y)
        def _():
            spread(t + 1, (xx,))

        multiply(t, n_grp // 2, n_grp)

        @pl.when(t > 1)
        def _():
            last_sums(t - 1)

        @pl.when(t + 1 < n_y)
        def _():
            share(t + 1)

        for k in range(2):
            for h in range(2):
                a_copy(t, k, h).wait_send()
            b_copy(t, k).wait_send()
        first_sums(t)

        @pl.when(t > 0)
        def _():
            early_sums(t)

        gather_back(t, (xx,))

        @pl.loop(0, n_grp)
        def _(i):
            p_copy(t, i).wait_send()

        @pl.when(t > 2)
        def _():
            give_back(t - 2, False)

    top = jnp.max(table[:, :, 0, packed:width])
    flags[0] = jnp.full((1, 128), top, jnp.int32)
    flag_copy().start()
    last_sums(n_y - 1)
    early_sums(0)
    last_sums(0)
    for t in range(1, n_y + 1):
        if n_y - 2 <= t < n_y:
            give_back(t, False)
        if t > 1:
            h_copy(t - 1).wait_recv()
            combine_into(t - 1, t == 2)
    flag_copy().wait()
    most_ref[...] = jnp.maximum(flags[0], flags[1])
    for t in range(1, n_y):
        list_copy(t).wait_send()
        y_copy(t).wait_send()
        h_copy(t).wait_send()

    @pl.loop(0, n_y)
    def _(t):
        for k in range(3):
            table_copy(t, k).wait_send()
        for k in range(2):
            e_copy(t, k).wait_send()
            n_copy(t, k).wait_send()
            f_copy(t, k).wait_send()

    give_back(0, True)
    combine_into(0, False)


def packed_layer(base, ids_loc, gate_loc, x_loc, wg, wu, wd, n_y, n_tp, packed, cap, collective_id):
    tok, d_model = x_loc.shape
    n_loc, _, hidden = wg.shape
    n_x = n_tp // 2
    n_grp = n_loc // GROUP
    half = halves(packed)[0]
    width = -(-(packed + 1) // 128) * 128
    dma = pltpu.SemaphoreType.DMA
    hbm = pl.BlockSpec(memory_space=pltpu.HBM)
    vmem = pl.BlockSpec(memory_space=pltpu.VMEM)
    return pl.pallas_call(
        functools.partial(packed_kernel, n_y, n_x, packed, cap),
        out_shape=(jax.ShapeDtypeStruct((tok, d_model), BF16), jax.ShapeDtypeStruct((1, 128), jnp.int32)),
        in_specs=[pl.BlockSpec(memory_space=pltpu.SMEM)] + [vmem] * 3 + [hbm] * 3,
        out_specs=(vmem, vmem),
        scratch_shapes=[
            pltpu.VMEM((n_y, packed, d_model), BF16),
            pltpu.VMEM((n_y, n_x, packed, d_model), BF16),
            pltpu.VMEM((2, n_loc, 2 * n_x, cap, d_model), BF16),
            pltpu.VMEM((2, n_loc, n_x, cap, d_model), BF16),
            pltpu.VMEM((2, n_y, half, d_model), BF16),
            pltpu.VMEM((2, n_y, packed, d_model), BF16),
            pltpu.VMEM((n_y, packed, d_model), BF16),
            pltpu.VMEM((W_SLOTS, GROUP, d_model, 2 * hidden), BF16),
            pltpu.VMEM((W_SLOTS, GROUP, hidden, d_model), BF16),
            pltpu.VMEM((tok, 128), F32),
            pltpu.VMEM((tok, 128), F32),
            pltpu.VMEM((n_y, 1, width), jnp.int32),
            pltpu.VMEM((n_y, n_x, 1, width), jnp.int32),
            pltpu.VMEM((2, 1, 128), jnp.int32),
            dma((n_y,)), dma((n_y,)), dma((n_y, 3)), dma((n_y, 3)), dma, dma,
            dma((n_y,)), dma((n_y,)),
            dma((n_y, 2, 2)), dma((n_y, 2, 2)),
            dma((n_y, 2)), dma((n_y, 2)),
            dma((n_y, n_x)), dma((n_y, n_x)),
            dma((n_y, n_grp)), dma((n_y, n_grp)),
            dma((n_y, 2)), dma((n_y, 2)),
            dma((n_y, 2)), dma((n_y, 2)),
            dma((n_y, 2)), dma((n_y, 2)),
            dma((n_y,)), dma((n_y,)),
            dma((W_SLOTS, 3)),
        ],
        compiler_params=pltpu.CompilerParams(
            collective_id=collective_id, has_side_effects=True, vmem_limit_bytes=VMEM_LIMIT
        ),
        name="packed_layer",
    )(base.reshape(1), ids_loc.reshape(1, tok), gate_loc.reshape(1, tok), x_loc, wg, wu, wd)


def solution(mesh):
    n_y, n_tp = mesh.shape["ep"], mesh.shape["tp"]
    row_spec = P(("dp", "ep", "tp"), None)

    def local_layer(x_loc, ids_loc, gate_loc, wg_loc, wu_loc, wd_loc):
        tok, d_model = x_loc.shape
        n_loc = wg_loc.shape[0]
        n_exp = n_loc * n_y
        capacity = CAP_FACTOR * tok // n_exp
        packed = n_loc * capacity * 19 // 32
        args = (ids_loc, gate_loc, x_loc, wg_loc, wu_loc, wd_loc, n_y, n_tp)
        out, most = packed_layer(jnp.int32(0), *args, packed, capacity, 0)

        def more(carry):
            total, base = carry
            extra, _ = packed_layer(base, *args, EXTRA, capacity, 1)
            return total + extra, base + EXTRA

        out, _ = lax.while_loop(lambda carry: carry[1] < most[0, 0], more, (out, jnp.int32(packed)))
        return out

    return jax.shard_map(local_layer, mesh=mesh, in_specs=(row_spec, row_spec, row_spec, P("ep", None, "tp"), P("ep", None, "tp"), P("ep", "tp", None)), out_specs=row_spec, check_vma=False)
```

time: 148 us -> 141 us (0.953)
  Pallas kernels: 144 us -> 138 us
  other arithmetic: 2.88 us -> 0 us
    pallas_call x1, Pallas kernels: 144 us -> 138 us  [packed_layer(): pl.pallas_call(functools.partial(packed_kernel, n_y, n_x, packed, cap), o...]
    convert_element_type x1 -> x0, other arithmetic: 2.88 us -> none  [local_layer(): return (picked.astype(F32) * gate_loc).astype(BF16)]
where the time goes in v5:
time: 141 us; the launch traced here: 140 us
  Pallas kernels  138 us (98%)
    pallas_call x1, Pallas kernels, packed_layer(): pl.pallas_call(functools.partial(packed_kernel, n_y, n_x, packed, cap), o...  138 us

profile of v5, /device:TPU:97, one launch (start us, length us, event | category | flops | bytes accessed | tf_op | source)
XLA Modules:
  0.0 140.5 jit_solution(4344558549107598728)
XLA Ops:
  0.0 0.0 copy-start
  0.0 0.0 copy-start.1
  0.0 0.0 copy-start.2
  0.0 138.5 %packed_layer.2 = (bf16[1024,768]{1,0:T(8,128)(2,1)S(1)}, s32[1,128]{1,0:T(1,128)}) custom-call(s32[1]{0:T(128)} %constant.1.clone.1.base_ref, s32[1,1024]{1,0:T(1,128)} %bitcast.15, f32[1,1024]{1,0:T(1,128)} %bitcast.17, bf16[1024,768]{1,0:T(8,128)(2,1)} %x_ref.1, bf16[16,768,384]{2,1,0:T(8,128)(2,1)} %wg_hbm.1, bf16[16,768,384]{2,1,0:T(8,128)(2,1)} %wu_hbm.1, ...), custom_call_target="tpu_custom_call" | custom-call | tf_op jit(solution)/shard_map/packed_layer/pallas_call | solution.py:439
  138.5 0.0 copy-done
  138.5 0.0 copy-done.1
  138.5 0.0 copy-done.2
  138.5 0.8 while.10
  139.3 1.1 copy.16
Async XLA Ops:
  0.0 138.5 %copy-start = (bf16[1024,768]{1,0:T(8,128)(2,1)S(1)}, bf16[1024,768]{1,0:T(8,128)(2,1)}, u32[]{:S(2)}) copy-start(bf16[1024,768]{1,0:T(8,128)(2,1)} %x_ref.1) | copy-start | bytes 4718596
  0.0 138.5 %copy-start.1 = (s32[1024,1]{0,1:T(1,128)S(1)}, s32[1024,1]{0,1:T(1,128)}, u32[]{:S(2)}) copy-start(s32[1024,1]{0,1:T(1,128)} %param.9) | copy-start | bytes 12292
  0.0 138.5 %copy-start.2 = (f32[1024,1]{0,1:T(1,128)S(1)}, f32[1024,1]{0,1:T(1,128)}, u32[]{:S(2)}) copy-start(f32[1024,1]{0,1:T(1,128)} %param.10) | copy-start | bytes 12292

commit v6 on v5

--- a/solution.py
+++ b/solution.py
@@ -23,8 +23,8 @@
 
 
 def packed_kernel(
-    n_y, n_x, packed, cap, base_ref, ids_ref, gate_ref, x_ref, wg_hbm, wu_hbm, wd_hbm, out_ref, most_ref,
-    pack_buf, x_buf, slot_buf, pair_buf, opp_buf, nbr_buf, ret_buf, w_in, w_out, pos_col, gate_col,
+    n_y, n_x, packed, cap, base_ref, ids_ref, gate_ref, x_hbm, wg_hbm, wu_hbm, wd_hbm, out_ref, most_ref,
+    x_ref, x_sem, pack_buf, x_buf, slot_buf, pair_buf, opp_buf, nbr_buf, ret_buf, w_in, w_out, pos_col, gate_col,
     lists, table, flags, l_send, l_recv, t_send, t_recv, m_send, m_recv, ys_send, ys_recv, a_send, a_recv, b_send, b_recv, s_send, s_recv,
     p_send, p_recv, e_send, e_recv, n_send, n_recv, f_send, f_recv, h_send, h_recv, w_sem,
 ):
@@ -136,6 +136,8 @@
             pltpu.make_async_copy(wd_hbm.at[at], w_out.at[s], w_sem.at[s, 2]),
         )
 
+    x_copy = pltpu.make_async_copy(x_hbm, x_ref, x_sem)
+    x_copy.start()
     barrier = pltpu.get_barrier_semaphore()
     for device in [right, left, across, mate] + [{"ep": (yy + d) % n_y} for d in range(1, n_y)]:
         pl.semaphore_signal(barrier, inc=1, device_id=device, device_id_type=MESH)
@@ -313,6 +315,7 @@
                 y = y + out_ref[rows, :].astype(F32)
             out_ref[rows, :] = y.astype(BF16)
 
+    x_copy.wait()
     x_buf[0, xx] = pack(0)
     pl.semaphore_wait(barrier, 3 + n_y)
     send_half(0, 0)
@@ -360,15 +363,15 @@
             s_copy(t, b).wait_send()
         multiply(t, 0, n_grp // 2)
 
+        @pl.when(t > 1)
+        def _():
+            last_sums(t - 1)
+
         @pl.when(t + 1 < n_y)
         def _():
             spread(t + 1, (xx,))
 
         multiply(t, n_grp // 2, n_grp)
-
-        @pl.when(t > 1)
-        def _():
-            last_sums(t - 1)
 
         @pl.when(t + 1 < n_y)
         def _():
@@ -439,9 +442,11 @@
     return pl.pallas_call(
         functools.partial(packed_kernel, n_y, n_x, packed, cap),
         out_shape=(jax.ShapeDtypeStruct((tok, d_model), BF16), jax.ShapeDtypeStruct((1, 128), jnp.int32)),
-        in_specs=[pl.BlockSpec(memory_space=pltpu.SMEM)] + [vmem] * 3 + [hbm] * 3,
+        in_specs=[pl.BlockSpec(memory_space=pltpu.SMEM)] + [vmem] * 2 + [hbm] * 4,
         out_specs=(vmem, vmem),
         scratch_shapes=[
+            pltpu.VMEM((tok, d_model), BF16),
+            dma,
             pltpu.VMEM((n_y, packed, d_model), BF16),
             pltpu.VMEM((n_y, n_x, packed, d_model), BF16),
             pltpu.VMEM((2, n_loc, 2 * n_x, cap, d_model), BF16),

time: 141 us -> 140 us (level)
  no operation moved by 1% of the time
where the time goes in v6:
time: 140 us
  Pallas kernels  138 us (99%)
    pallas_call x1, Pallas kernels, packed_layer(): pl.pallas_call(functools.partial(packed_kernel, n_y, n_x, packed, cap), o...  138 us

profile of v6, /device:TPU:97, one launch (start us, length us, event | category | flops | bytes accessed | tf_op | source)
XLA Modules:
  0.0 140.2 jit_solution(13805713809626193511)
XLA Ops:
  0.0 0.0 copy-start
  0.0 0.0 copy-start.1
  0.0 0.0 copy-start.2
  0.0 138.2 %packed_layer.2 = (bf16[1024,768]{1,0:T(8,128)(2,1)S(1)}, s32[1,128]{1,0:T(1,128)}) custom-call(s32[1]{0:T(128)} %constant.1.clone.1.base_ref, s32[1,1024]{1,0:T(1,128)} %bitcast.15, f32[1,1024]{1,0:T(1,128)} %bitcast.17, bf16[1024,768]{1,0:T(8,128)(2,1)} %x_hbm.1, bf16[16,768,384]{2,1,0:T(8,128)(2,1)} %wg_hbm.1, bf16[16,768,384]{2,1,0:T(8,128)(2,1)} %wu_hbm.1, ...), custom_call_target="tpu_custom_call" | custom-call | tf_op jit(solution)/shard_map/packed_layer/pallas_call | solution.py:442
  138.2 0.0 copy-done
  138.2 0.0 copy-done.1
  138.3 0.0 copy-done.2
  138.3 0.8 while.10
  139.1 1.1 copy.16
Async XLA Ops:
  0.0 138.2 %copy-start = (bf16[1024,768]{1,0:T(8,128)(2,1)S(1)}, bf16[1024,768]{1,0:T(8,128)(2,1)}, u32[]{:S(2)}) copy-start(bf16[1024,768]{1,0:T(8,128)(2,1)} %x_hbm.1) | copy-start | bytes 4718596
  0.0 138.2 %copy-start.1 = (s32[1024,1]{0,1:T(1,128)S(1)}, s32[1024,1]{0,1:T(1,128)}, u32[]{:S(2)}) copy-start(s32[1024,1]{0,1:T(1,128)} %param.9) | copy-start | bytes 12292
  0.0 138.3 %copy-start.2 = (f32[1024,1]{0,1:T(1,128)S(1)}, f32[1024,1]{0,1:T(1,128)}, u32[]{:S(2)}) copy-start(f32[1024,1]{0,1:T(1,128)} %param.10) | copy-start | bytes 12292

commit v7 on v6

--- a/solution.py
+++ b/solution.py
@@ -279,36 +279,43 @@
         for k in range(2):
             n_copy(t, k).start()
 
+    def last_sum(t, k):
+        e_copy(t, k).wait_recv()
+        at = (t, ahead[k], part(k))
+        x_buf[at] = (x_buf[at].astype(F32) + opp_buf[k, t, pl.ds(0, sizes[k])].astype(F32)).astype(BF16)
+        f_copy(t, k).start()
+
     def last_sums(t):
         for k in range(2):
-            e_copy(t, k).wait_recv()
-            at = (t, ahead[k], part(k))
-            x_buf[at] = (x_buf[at].astype(F32) + opp_buf[k, t, pl.ds(0, sizes[k])].astype(F32)).astype(BF16)
-            f_copy(t, k).start()
-
-    def give_back(t, local):
+            last_sum(t, k)
+
+    def give_back(t):
         for k in range(2):
             n_copy(t, k).wait_recv()
             f_copy(t, k).wait_recv()
         total = x_buf[t, xx].astype(F32) + (nbr_buf[0, t].astype(F32) + nbr_buf[1, t].astype(F32))
-        if local:
-            ret_buf[t] = total.astype(BF16)
-        else:
-            x_buf[t, xx] = total.astype(BF16)
-            h_copy(t).start()
-
-    def combine_into(t, first):
+        x_buf[t, xx] = total.astype(BF16)
+        h_copy(t).start()
+
+    def keep_half(h):
+        f_copy(0, h).wait_recv()
+        n_copy(0, 1 - h).wait_recv()
+        at = part(h)
+        total = x_buf[0, xx, at].astype(F32) + (nbr_buf[0, 0, at].astype(F32) + nbr_buf[1, 0, at].astype(F32))
+        ret_buf[0, at] = total.astype(BF16)
+
+    def combine_into(t, first, low, size):
         tile = 256
 
         @pl.loop(0, tok // tile)
         def _(i):
             rows = pl.ds(pl.multiple_of(i * tile, tile), tile)
-            want = pos_col[rows, :] - (row_to(t) * packed).astype(F32)
+            want = pos_col[rows, :] - (row_to(t) * packed + low).astype(F32)
             lane = lax.broadcasted_iota(jnp.int32, (tile, 128), 1).astype(F32)
             pick = jnp.concatenate(
-                [(want == lane + float(128 * m)).astype(F32) for m in range(-(-packed // 128))], axis=1
+                [(want == lane + float(128 * m)).astype(F32) for m in range(-(-size // 128))], axis=1
             )
-            y = jnp.dot(pick[:, :packed].astype(BF16), ret_buf[t], preferred_element_type=F32)
+            y = jnp.dot(pick[:, :size].astype(BF16), ret_buf[t, pl.ds(low, size)], preferred_element_type=F32)
             gate = gate_col[rows, :]
             y = jnp.concatenate([y[:, m * 128:(m + 1) * 128] * gate for m in range(d_model // 128)], axis=1)
             if not first:
@@ -395,20 +402,22 @@
 
         @pl.when(t > 2)
         def _():
-            give_back(t - 2, False)
+            give_back(t - 2)
 
     top = jnp.max(table[:, :, 0, packed:width])
     flags[0] = jnp.full((1, 128), top, jnp.int32)
     flag_copy().start()
     last_sums(n_y - 1)
-    early_sums(0)
-    last_sums(0)
+    last_sum(0, 0)
+    for k in (1, 0):
+        n_copy(0, k).start()
+    last_sum(0, 1)
     for t in range(1, n_y + 1):
         if n_y - 2 <= t < n_y:
-            give_back(t, False)
+            give_back(t)
         if t > 1:
             h_copy(t - 1).wait_recv()
-            combine_into(t - 1, t == 2)
+            combine_into(t - 1, t == 2, 0, packed)
     flag_copy().wait()
     most_ref[...] = jnp.maximum(flags[0], flags[1])
     for t in range(1, n_y):
@@ -425,8 +434,9 @@
             n_copy(t, k).wait_send()
             f_copy(t, k).wait_send()
 
-    give_back(0, True)
-    combine_into(0, False)
+    for h in range(2):
+        keep_half(h)
+        combine_into(0, False, h * sizes[0], sizes[h])
 
 
 def packed_layer(base, ids_loc, gate_loc, x_loc, wg, wu, wd, n_y, n_tp, packed, cap, collective_id):
@@ -498,7 +508,10 @@
             extra, _ = packed_layer(base, *args, EXTRA, capacity, 1)
             return total + extra, base + EXTRA
 
-        out, _ = lax.while_loop(lambda carry: carry[1] < most[0, 0], more, (out, jnp.int32(packed)))
+        def passes(first):
+            return lax.while_loop(lambda carry: carry[1] < most[0, 0], more, (first, jnp.int32(packed)))[0]
+
+        out = lax.cond(most[0, 0] > packed, passes, lambda first: first, out)
         return out
 
     return jax.shard_map(local_layer, mesh=mesh, in_specs=(row_spec, row_spec, row_spec, P("ep", None, "tp"), P("ep", None, "tp"), P("ep", "tp", None)), out_specs=row_spec, check_vma=False)

time: 140 us -> 140 us (level)
  no operation moved by 1% of the time
where the time goes in v7:
time: 140 us
  Pallas kernels  139 us (99%)
    pallas_call x1, Pallas kernels, packed_layer(): pl.pallas_call(functools.partial(packed_kernel, n_y, n_x, packed, cap), o...  139 us

profile of v7, /device:TPU:97, one launch (start us, length us, event | category | flops | bytes accessed | tf_op | source)
XLA Modules:
  0.0 140.1 jit_solution(16200276242075883979)
XLA Ops:
  0.0 0.0 copy-start
  0.0 0.0 copy-start.1
  0.0 0.0 copy-start.2
  0.0 138.6 %packed_layer.2 = (bf16[1024,768]{1,0:T(8,128)(2,1)S(1)}, s32[1,128]{1,0:T(1,128)S(1)}) custom-call(s32[1]{0:T(128)} %constant.3.clone.1.base_ref, s32[1,1024]{1,0:T(1,128)} %bitcast.17, f32[1,1024]{1,0:T(1,128)} %bitcast.19, bf16[1024,768]{1,0:T(8,128)(2,1)} %x_hbm.1, bf16[16,768,384]{2,1,0:T(8,128)(2,1)} %wg_hbm.1, bf16[16,768,384]{2,1,0:T(8,128)(2,1)} %wu_hbm.1, ...), custom_call_target="tpu_custom_call" | custom-call | tf_op jit(solution)/shard_map/packed_layer/pallas_call | solution.py:452
  138.7 0.0 copy-done
  138.7 0.0 copy-done.1
  138.7 0.0 copy-done.2
  138.7 0.2 conditional.1
  138.9 1.1 copy.20
Async XLA Ops:
  0.0 138.7 %copy-start = (bf16[1024,768]{1,0:T(8,128)(2,1)S(1)}, bf16[1024,768]{1,0:T(8,128)(2,1)}, u32[]{:S(2)}) copy-start(bf16[1024,768]{1,0:T(8,128)(2,1)} %x_hbm.1) | copy-start | bytes 4718596
  0.0 138.7 %copy-start.1 = (s32[1024,1]{0,1:T(1,128)S(1)}, s32[1024,1]{0,1:T(1,128)}, u32[]{:S(2)}) copy-start(s32[1024,1]{0,1:T(1,128)} %param.11) | copy-start | bytes 12292
  0.0 138.7 %copy-start.2 = (f32[1024,1]{0,1:T(1,128)S(1)}, f32[1024,1]{0,1:T(1,128)}, u32[]{:S(2)}) copy-start(f32[1024,1]{0,1:T(1,128)} %param.12) | copy-start | bytes 12292

commit v8 on v7

--- a/solution.py
+++ b/solution.py
@@ -304,7 +304,7 @@
         total = x_buf[0, xx, at].astype(F32) + (nbr_buf[0, 0, at].astype(F32) + nbr_buf[1, 0, at].astype(F32))
         ret_buf[0, at] = total.astype(BF16)
 
-    def combine_into(t, first, low, size):
+    def combine_into(t, low, size):
         tile = 256
 
         @pl.loop(0, tok // tile)
@@ -318,9 +318,7 @@
             y = jnp.dot(pick[:, :size].astype(BF16), ret_buf[t, pl.ds(low, size)], preferred_element_type=F32)
             gate = gate_col[rows, :]
             y = jnp.concatenate([y[:, m * 128:(m + 1) * 128] * gate for m in range(d_model // 128)], axis=1)
-            if not first:
-                y = y + out_ref[rows, :].astype(F32)
-            out_ref[rows, :] = y.astype(BF16)
+            out_ref[rows, :] = (y + out_ref[rows, :].astype(F32)).astype(BF16)
 
     x_copy.wait()
     x_buf[0, xx] = pack(0)
@@ -348,6 +346,7 @@
         pos_col[i * tile:(i + 1) * tile, :] = jnp.transpose(jnp.broadcast_to(spot, (128, tile)))
         gate = gate_ref[:, i * tile:(i + 1) * tile]
         gate_col[i * tile:(i + 1) * tile, :] = jnp.transpose(jnp.broadcast_to(gate, (128, tile)))
+    out_ref[...] = jnp.zeros_like(out_ref)
     share(0)
 
     @pl.loop(0, n_y)
@@ -412,12 +411,16 @@
     for k in (1, 0):
         n_copy(0, k).start()
     last_sum(0, 1)
-    for t in range(1, n_y + 1):
-        if n_y - 2 <= t < n_y:
+    for t in range(1, n_y):
+        if t >= n_y - 2:
             give_back(t)
         if t > 1:
             h_copy(t - 1).wait_recv()
-            combine_into(t - 1, t == 2, 0, packed)
+            combine_into(t - 1, 0, packed)
+    keep_half(0)
+    combine_into(0, 0, sizes[0])
+    h_copy(n_y - 1).wait_recv()
+    combine_into(n_y - 1, 0, packed)
     flag_copy().wait()
     most_ref[...] = jnp.maximum(flags[0], flags[1])
     for t in range(1, n_y):
@@ -434,9 +437,8 @@
             n_copy(t, k).wait_send()
             f_copy(t, k).wait_send()
 
-    for h in range(2):
-        keep_half(h)
-        combine_into(0, False, h * sizes[0], sizes[h])
+    keep_half(1)
+    combine_into(0, sizes[0], sizes[1])
 
 
 def packed_layer(base, ids_loc, gate_loc, x_loc, wg, wu, wd, n_y, n_tp, packed, cap, collective_id):

time: 140 us -> 139 us (level)
  no operation moved by 1% of the time
where the time goes in v8:
time: 139 us
  Pallas kernels  138 us (99%)
    pallas_call x1, Pallas kernels, packed_layer(): pl.pallas_call(functools.partial(packed_kernel, n_y, n_x, packed, cap), o...  138 us

profile of v8, /device:TPU:97, one launch (start us, length us, event | category | flops | bytes accessed | tf_op | source)
XLA Modules:
  0.0 139.0 jit_solution(4900710415056761865)
XLA Ops:
  0.0 0.0 copy-start
  0.0 0.0 copy-start.1
  0.0 0.0 copy-start.2
  0.0 137.5 %packed_layer.2 = (bf16[1024,768]{1,0:T(8,128)(2,1)S(1)}, s32[1,128]{1,0:T(1,128)S(1)}) custom-call(s32[1]{0:T(128)} %constant.3.clone.1.base_ref, s32[1,1024]{1,0:T(1,128)} %bitcast.17, f32[1,1024]{1,0:T(1,128)} %bitcast.19, bf16[1024,768]{1,0:T(8,128)(2,1)} %x_hbm.1, bf16[16,768,384]{2,1,0:T(8,128)(2,1)} %wg_hbm.1, bf16[16,768,384]{2,1,0:T(8,128)(2,1)} %wu_hbm.1, ...), custom_call_target="tpu_custom_call" | custom-call | tf_op jit(solution)/shard_map/packed_layer/pallas_call | solution.py:454
  137.6 0.0 copy-done
  137.6 0.0 copy-done.1
  137.6 0.0 copy-done.2
  137.6 0.2 conditional.1
  137.8 1.1 copy.20
Async XLA Ops:
  0.0 137.6 %copy-start = (bf16[1024,768]{1,0:T(8,128)(2,1)S(1)}, bf16[1024,768]{1,0:T(8,128)(2,1)}, u32[]{:S(2)}) copy-start(bf16[1024,768]{1,0:T(8,128)(2,1)} %x_hbm.1) | copy-start | bytes 4718596
  0.0 137.6 %copy-start.1 = (s32[1024,1]{0,1:T(1,128)S(1)}, s32[1024,1]{0,1:T(1,128)}, u32[]{:S(2)}) copy-start(s32[1024,1]{0,1:T(1,128)} %param.11) | copy-start | bytes 12292
  0.0 137.6 %copy-start.2 = (f32[1024,1]{0,1:T(1,128)S(1)}, f32[1024,1]{0,1:T(1,128)}, u32[]{:S(2)}) copy-start(f32[1024,1]{0,1:T(1,128)} %param.12) | copy-start | bytes 12292
